TPU v7x, 32 devices: a whole 2x2x4 slice. The times are simulated.
32 devices in a mesh: dp: 16 (over z, y, core), tp: 2 (over x).
Axes of the slice: x: 2, y: 2, z: 4, core: 2. Of those that a mesh axis runs over, the one named last changes fastest.
Arguments:
- hidden: bfloat16 [4096, 4096], P(('dp', 'tp')), may hold values from -6 to 6
- query_grad: bfloat16 [4096, 1024], P('dp', 'tp'), may hold values from -1.5 to 1.5
- key_grad: bfloat16 [4096, 256], P('dp', 'tp'), may hold values from -1.5 to 1.5
- value_grad: bfloat16 [4096, 256], P('dp', 'tp'), may hold values from -1.5 to 1.5
- w_query: bfloat16 [4096, 1024], P(None, 'tp'), may hold values from -0.09375 to 0.09375
- w_key: bfloat16 [4096, 256], P(None, 'tp'), may hold values from -0.09375 to 0.09375
- w_value: bfloat16 [4096, 256], P(None, 'tp'), may hold values from -0.09375 to 0.09375
Outputs:
- hidden_grad: bfloat16 [4096, 4096], P(('dp', 'tp'))
- grad_query: float32 [4096, 1024], P('dp', 'tp')
- grad_key: float32 [4096, 256], P('dp', 'tp')
- grad_value: float32 [4096, 256], P('dp', 'tp')
All inputs are finite; a program needn't handle non-finite values.
Results may differ from a plain program's by a relative error of at most 0.014.
Values may be sent and summed in bfloat16 or wider, within the bound.
A program may use at most 256 MiB of HBM per device.

v0:
```python
import functools

import jax
import jax.numpy as jnp
from jax import lax
from jax.experimental import pallas as pl
from jax.experimental.pallas import tpu as pltpu
from jax.sharding import PartitionSpec as P

MESH = pl.DeviceIdType.MESH


def contract_rows(left, right):
    return lax.dot_general(
        left, right, (((0,), (0,)), ((), ())), preferred_element_type=jnp.float32
    )


def contract_cols(left, right):
    return lax.dot_general(
        left, right, (((1,), (1,)), ((), ())), preferred_element_type=jnp.float32
    )


def local(hidden, query_grad, key_grad, value_grad, w_query, w_key, w_value):
    query_width = w_query.shape[1]
    head_width = w_key.shape[1]
    all_grads = jnp.concatenate((query_grad, key_grad, value_grad), axis=1)
    all_weights = jnp.concatenate((w_query, w_key, w_value), axis=1)
    total = contract_rows(lax.all_gather(hidden, "tp", axis=0, tiled=True), all_grads)
    summed = lax.psum_scatter(
        contract_cols(all_grads, all_weights).astype(jnp.bfloat16),
        "tp",
        scatter_dimension=0,
        tiled=True,
    )
    weight_grad = lax.psum_scatter(
        total.astype(jnp.bfloat16), "dp", scatter_dimension=0, tiled=True
    ).astype(jnp.float32)
    grad_query = weight_grad[:, :query_width]
    grad_key = weight_grad[:, query_width : query_width + head_width]
    grad_value = weight_grad[:, query_width + head_width :]
    return (summed, grad_query, grad_key, grad_value)


def kernel(
    n_z, pieces,
    hidden, query_grad, key_grad, value_grad, w_query, w_key, w_value,
    result, final,
    tokens, grads, weights, head_out, head_in, core_out, core_in,
    y_out, y_in, total, z_out, z_in, own_head,
    load_sem, tok_send, tok_recv, head_send, head_recv, core_send, core_recv,
    y_send, y_recv, z_send, z_recv,
):
    dp = lax.axis_index("dp")
    tp = lax.axis_index("tp")
    core = lax.rem(dp, 2)
    y = lax.rem(dp // 2, 2)
    z = dp // 4
    half = hidden.shape[0]
    q_w = query_grad.shape[1]
    k_w = key_grad.shape[1]
    rows = final.shape[0]
    pair = 2 * rows
    width = hidden.shape[1] // pieces

    x_peer = (dp, 1 - tp)
    core_peer = (dp + 1 - 2 * core, tp)
    y_peer = (dp + 2 - 4 * y, tp)
    far_first = sorted(range(1, n_z), key=lambda o: -min(o, n_z - o)) + [0]
    z_of = [lax.rem(z + o, n_z) for o in far_first]

    def z_peer(k):
        return (z_of[k] * 4 + y * 2 + core, tp)

    mine = pl.ds(pl.multiple_of(tp * half, half), half)
    theirs = pl.ds(pl.multiple_of((1 - tp) * half, half), half)

    def load(index, source, target):
        copy = pltpu.make_async_copy(source, target, load_sem.at[index])
        copy.start()
        return copy

    loads = [
        load(0, query_grad, grads.at[:, pl.ds(0, q_w)]),
        load(1, key_grad, grads.at[:, pl.ds(q_w, k_w)]),
        load(2, value_grad, grads.at[:, pl.ds(q_w + k_w, k_w)]),
        load(3, hidden, tokens.at[mine, :]),
        load(4, w_query, weights.at[:, pl.ds(0, q_w)]),
        load(5, w_key, weights.at[:, pl.ds(q_w, k_w)]),
        load(6, w_value, weights.at[:, pl.ds(q_w + k_w, k_w)]),
    ]

    barrier = pltpu.get_barrier_semaphore()
    peers = [x_peer, core_peer, y_peer] + [z_peer(k) for k in range(n_z - 1)]
    for peer in peers:
        pl.semaphore_signal(barrier, inc=1, device_id=peer, device_id_type=MESH)
    pl.semaphore_wait(barrier, len(peers))

    def remote(source, target, send, recv, peer):
        return pltpu.make_async_remote_copy(
            src_ref=source, dst_ref=target, send_sem=send, recv_sem=recv,
            device_id=peer, device_id_type=MESH,
        )

    def pair_of(k):
        return z_of[k // 2] * 2 + (1 - y if k % 2 == 0 else y)

    n_pairs = 2 * n_z
    tok_copies = []
    for k in range(n_pairs):
        columns = pl.ds(pl.multiple_of(pair_of(k) * pair, pair), pair)
        copy = remote(
            hidden.at[:, columns], tokens.at[mine, columns],
            tok_send.at[k], tok_recv.at[k], x_peer,
        )
        copy.start()
        tok_copies.append(copy)

    for copy in loads[:4]:
        copy.wait()

    head_copies = [
        remote(
            head_out.at[j], head_in.at[j], head_send.at[j], head_recv.at[j], x_peer
        )
        for j in range(pieces)
    ]
    core_copies = [
        remote(
            core_out.at[k], core_in.at[k], core_send.at[k], core_recv.at[k], core_peer
        )
        for k in range(n_pairs)
    ]
    y_copies = [
        [
            remote(
                y_out.at[k, h], y_in.at[k, h],
                y_send.at[k, h], y_recv.at[k, h], y_peer,
            )
            for h in range(2)
        ]
        for k in range(n_z)
    ]
    z_copies = [
        [
            remote(
                z_out.at[k, h], z_in.at[k, h],
                z_send.at[k, h], z_recv.at[k, h], z_peer(k),
            )
            for h in range(2)
        ]
        for k in range(n_z - 1)
    ]
    part = rows // 2

    def block(k, which, first, size):
        start = pl.multiple_of(pair_of(k) * pair + which * rows + first, part)
        return contract_rows(tokens[:, pl.ds(start, size)], grads[...])

    def finish(k):
        for h in range(2):
            own = block(k, core, h * part, part)
            if h == 0:
                core_copies[k].wait_recv()
            span = pl.ds(h * part, part)
            summed = own + core_in[k, span].astype(jnp.float32)
            if k % 2 == 0:
                y_out[k // 2, h] = summed.astype(y_out.dtype)
                y_copies[k // 2][h].start()
            else:
                total[k // 2, h] = summed

    def head_piece(j):
        columns = pl.ds(j * width, width)
        head_out[j] = contract_cols(
            grads[theirs, :], weights[columns, :]
        ).astype(head_out.dtype)
        head_copies[j].start()
        own_head[:, columns] = contract_cols(grads[mine, :], weights[columns, :])

    def forward(k, h):
        y_copies[k][h].wait_recv()
        summed = total[k, h] + y_in[k, h].astype(jnp.float32)
        if k < n_z - 1:
            z_out[k, h] = summed.astype(z_out.dtype)
            z_copies[k][h].start()
        else:
            total[k, h] = summed

    sent = 0
    for k in range(n_pairs):
        tok_copies[k].wait_recv()
        core_out[k] = block(k, 1 - core, 0, rows).astype(core_out.dtype)
        core_copies[k].start()
        finish(k)
        if k == 0:
            for copy in loads[4:]:
                copy.wait()
        head_piece(k)
        if k >= 1 and k % 3 != 2:
            forward(sent // 2, sent % 2)
            sent += 1
    assert pieces == n_pairs

    def add_heads(j):
        head_copies[j].wait_recv()
        columns = pl.ds(j * width, width)
        own = own_head[:, columns]
        result[:, columns] = (own + head_in[j].astype(jnp.float32)).astype(result.dtype)

    ready = 0
    for step in range(sent, 2 * n_z):
        forward(step // 2, step % 2)
        stop = (pieces - 1) * (step + 1 - sent) // (2 * n_z - sent)
        for j in range(ready, stop):
            add_heads(j)
        ready = stop
    for h in range(2):
        span = pl.ds(h * part, part)
        summed = total[n_z - 1, h]
        for s in range(n_z - 1):
            z_copies[s][h].wait_recv()
            summed = summed + z_in[s, h].astype(jnp.float32)
        final[span, :] = summed
    for j in range(ready, pieces):
        add_heads(j)
    flat = [copy for pair in y_copies + z_copies for copy in pair]
    for copy in tok_copies + head_copies + core_copies + flat:
        copy.wait_send()


def place(result, final, out_hidden, out_query, out_key, out_value, sem):
    q_w, k_w = out_query.shape[1], out_key.shape[1]
    copies = [
        pltpu.make_async_copy(result, out_hidden, sem.at[0]),
        pltpu.make_async_copy(final.at[:, pl.ds(0, q_w)], out_query, sem.at[1]),
        pltpu.make_async_copy(final.at[:, pl.ds(q_w, k_w)], out_key, sem.at[2]),
        pltpu.make_async_copy(
            final.at[:, pl.ds(q_w + k_w, k_w)], out_value, sem.at[3]
        ),
    ]
    for copy in copies:
        copy.start()
    for copy in copies:
        copy.wait()


def fused(n_dp, hidden, query_grad, key_grad, value_grad, w_query, w_key, w_value):
    half, depth = hidden.shape
    group = query_grad.shape[0]
    q_w, k_w = w_query.shape[1], w_key.shape[1]
    wide = q_w + 2 * k_w
    rows = depth // n_dp
    n_z = n_dp // 4
    n_pairs = 2 * n_z
    pieces = n_pairs
    width = depth // pieces
    bf16, f32 = jnp.bfloat16, jnp.float32
    dma = pltpu.SemaphoreType.DMA
    held = pl.pallas_call(
        functools.partial(kernel, n_z, pieces),
        out_shape=(pltpu.VMEM((half, depth), bf16), pltpu.VMEM((rows, wide), f32)),
        in_specs=[pl.BlockSpec(memory_space=pl.ANY)] * 7,
        out_specs=(pl.BlockSpec(memory_space=pltpu.VMEM),) * 2,
        scratch_shapes=[
            pltpu.VMEM((group, depth), bf16),
            pltpu.VMEM((group, wide), bf16),
            pltpu.VMEM((depth, wide), bf16),
            pltpu.VMEM((pieces, half, width), bf16),
            pltpu.VMEM((pieces, half, width), bf16),
            pltpu.VMEM((n_pairs, rows, wide), bf16),
            pltpu.VMEM((n_pairs, rows, wide), bf16),
            pltpu.VMEM((n_z, 2, rows // 2, wide), bf16),
            pltpu.VMEM((n_z, 2, rows // 2, wide), bf16),
            pltpu.VMEM((n_z, 2, rows // 2, wide), f32),
            pltpu.VMEM((n_z - 1, 2, rows // 2, wide), bf16),
            pltpu.VMEM((n_z - 1, 2, rows // 2, wide), bf16),
            pltpu.VMEM((half, depth), f32),
            dma((7,)),
            dma((n_pairs,)), dma((n_pairs,)),
            dma((pieces,)), dma((pieces,)),
            dma((n_pairs,)), dma((n_pairs,)),
            dma((n_z, 2)), dma((n_z, 2)),
            dma((n_z - 1, 2)), dma((n_z - 1, 2)),
        ],
        compiler_params=pltpu.CompilerParams(
            collective_id=0, has_side_effects=True, vmem_limit_bytes=56 * 1024 * 1024
        ),
    )(hidden, query_grad, key_grad, value_grad, w_query, w_key, w_value)
    return pl.pallas_call(
        place,
        out_shape=(
            jax.ShapeDtypeStruct((half, depth), bf16),
            jax.ShapeDtypeStruct((rows, q_w), f32),
            jax.ShapeDtypeStruct((rows, k_w), f32),
            jax.ShapeDtypeStruct((rows, k_w), f32),
        ),
        in_specs=[pl.BlockSpec(memory_space=pltpu.VMEM)] * 2,
        out_specs=(pl.BlockSpec(memory_space=pl.ANY),) * 4,
        scratch_shapes=[dma((4,))],
    )(*[pltpu.with_memory_space_constraint(a, pltpu.VMEM) for a in held])


def solution(mesh):
    placed = (
        P(("dp", "tp"), None),
        P("dp", "tp"),
        P("dp", "tp"),
        P("dp", "tp"),
        P(None, "tp"),
        P(None, "tp"),
        P(None, "tp"),
    )
    n_dp, n_tp = mesh.shape["dp"], mesh.shape["tp"]
    body = local
    if n_tp == 2 and n_dp % 4 == 0 and n_dp > 4:
        body = functools.partial(fused, n_dp)
    return jax.shard_map(
        body,
        mesh=mesh,
        in_specs=placed,
        out_specs=(P(("dp", "tp"), None), P("dp", "tp"), P("dp", "tp"), P("dp", "tp")),
        check_vma=False,
    )
```

profile of v0, /device:TPU:0, one launch (start us, length us, event | category | flops | bytes accessed | tf_op | source)
XLA Modules:
  0.0 56.6 jit_solution(15663341265545791674)
XLA Ops:
  0.6 54.7 %shard_map.102 = (bf16[128,4096]{1,0:T(8,128)(2,1)S(1)}, f32[256,768]{1,0:T(8,128)S(1)}) custom-call(bf16[128,4096]{1,0:T(8,128)(2,1)} %hidden.1, bf16[256,512]{1,0:T(8,128)(2,1)} %query_grad.1, bf16[256,128]{1,0:T(8,128)(2,1)} %key_grad.1, bf16[256,128]{1,0:T(8,128)(2,1)} %value_grad.1, bf16[4096,512]{1,0:T(8,128)(2,1)} %w_query.1, ...), custom_call_target="tpu_custom_call" | custom-call | tf_op jit(solution)/shard_map/pallas_call | solution.py:261
  55.3 1.3 %shard_map.103 = (bf16[128,4096]{1,0:T(8,128)(2,1)}, f32[256,512]{1,0:T(8,128)}, f32[256,128]{1,0:T(8,128)}, f32[256,128]{1,0:T(8,128)}) custom-call(bf16[128,4096]{1,0:T(8,128)(2,1)S(1)} %get-tuple-element.6.result, f32[256,768]{1,0:T(8,128)S(1)} %get-tuple-element.7.final), custom_call_target="tpu_custom_call" | custom-call | tf_op jit(solution)/shard_map/pallas_call | solution.py:291
where the time goes:
time: 56.7 us; the launch traced here: 56.6 us
  Pallas kernels  55.9 us (99%)
  between operations  0.64 us (1%)
    pallas_call x1, Pallas kernels, fused(): pl.pallas_call(functools.partial(kernel, n_z, pieces), out_shape=(pltpu.V...  54.7 us
    pallas_call x1, Pallas kernels, fused(): pl.pallas_call(place, out_shape=(jax.ShapeDtypeStruct((half, depth), bf16...  1.25 us

commit v1 on v0

v1 whole, which is shorter than its diff:
```python
import functools

import jax
import jax.numpy as jnp
from jax import lax
from jax.experimental import pallas as pl
from jax.experimental.pallas import tpu as pltpu
from jax.sharding import PartitionSpec as P

MESH = pl.DeviceIdType.MESH


def contract_rows(left, right):
    return lax.dot_general(
        left, right, (((0,), (0,)), ((), ())), preferred_element_type=jnp.float32
    )


def contract_cols(left, right):
    return lax.dot_general(
        left, right, (((1,), (1,)), ((), ())), preferred_element_type=jnp.float32
    )


def local(hidden, query_grad, key_grad, value_grad, w_query, w_key, w_value):
    query_width = w_query.shape[1]
    head_width = w_key.shape[1]
    all_grads = jnp.concatenate((query_grad, key_grad, value_grad), axis=1)
    all_weights = jnp.concatenate((w_query, w_key, w_value), axis=1)
    total = contract_rows(lax.all_gather(hidden, "tp", axis=0, tiled=True), all_grads)
    summed = lax.psum_scatter(
        contract_cols(all_grads, all_weights).astype(jnp.bfloat16),
        "tp",
        scatter_dimension=0,
        tiled=True,
    )
    weight_grad = lax.psum_scatter(
        total.astype(jnp.bfloat16), "dp", scatter_dimension=0, tiled=True
    ).astype(jnp.float32)
    grad_query = weight_grad[:, :query_width]
    grad_key = weight_grad[:, query_width : query_width + head_width]
    grad_value = weight_grad[:, query_width + head_width :]
    return (summed, grad_query, grad_key, grad_value)


def targets(n_z, z):
    near_low = z < n_z - 1 - z
    return sorted(
        range(n_z), key=lambda t: (-abs(t - z), t if near_low else -t)
    )


def pick(values, index):
    chosen = jnp.int32(values[0])
    for i, value in enumerate(values[1:]):
        chosen = jnp.where(index == i + 1, jnp.int32(value), chosen)
    return chosen


def kernel(
    n_z, pieces, n_c,
    hidden, query_grad, key_grad, value_grad, w_query, w_key, w_value,
    result, final,
    tokens, grads, weights, head_out, head_in, core_out, core_in,
    total, z_out, z_in, own_head,
    load_sem, own_send, own_recv, fwd_send, fwd_recv, ytok_send, ytok_recv,
    ygrad_send, ygrad_recv, head_send, head_recv, core_send, core_recv,
    z_send, z_recv,
):
    dp = lax.axis_index("dp")
    tp = lax.axis_index("tp")
    core = lax.rem(dp, 2)
    y = lax.rem(dp // 2, 2)
    z = dp // 4
    half = hidden.shape[0]
    group = query_grad.shape[0]
    q_w = query_grad.shape[1]
    k_w = key_grad.shape[1]
    rows = final.shape[0]
    pair = 2 * rows
    width = hidden.shape[1] // pieces
    chunk = 2 * k_w
    bf16, f32 = jnp.bfloat16, jnp.float32

    x_peer = (dp, 1 - tp)
    core_peer = (dp + 1 - 2 * core, tp)
    y_peer = (dp + 2 - 4 * y, tp)
    at_low, at_high = z == 0, z == n_z - 1
    at_end = jnp.logical_or(at_low, at_high)

    order = [targets(n_z, i) for i in range(n_z)]
    target = [pick([order[i][k] for i in range(n_z)], z) for k in range(n_z)]
    down = [jnp.where(target[k] < z, 1, 0) for k in range(n_z)]

    mine = pl.ds(pl.multiple_of(tp * half, half), half)
    theirs = pl.ds(pl.multiple_of((1 - tp) * half, half), half)
    mine_far = pl.ds(pl.multiple_of(group + tp * half, half), half)

    def columns_of(k, side):
        return pl.ds(pl.multiple_of((target[k] * 2 + side) * pair, pair), pair)

    def load(index, source, place):
        copy = pltpu.make_async_copy(source, place, load_sem.at[index])
        copy.start()
        return copy

    near = pl.ds(0, group)
    far = pl.ds(group, group)
    grad_loads = [
        load(0, query_grad, grads.at[near, pl.ds(0, q_w)]),
        load(1, key_grad, grads.at[near, pl.ds(q_w, k_w)]),
        load(2, value_grad, grads.at[near, pl.ds(q_w + k_w, k_w)]),
    ]
    weight_loads = [
        load(3, w_query, weights.at[:, pl.ds(0, q_w)]),
        load(4, w_key, weights.at[:, pl.ds(q_w, k_w)]),
        load(5, w_value, weights.at[:, pl.ds(q_w + k_w, k_w)]),
    ]
    token_loads = [
        load(6 + k, hidden.at[:, columns_of(k, y)], tokens.at[k, mine, :])
        for k in range(n_z)
    ]

    barrier = pltpu.get_barrier_semaphore()

    def greet(peer):
        pl.semaphore_signal(barrier, inc=1, device_id=peer, device_id_type=MESH)

    for peer in (x_peer, y_peer, core_peer):
        greet(peer)

    @pl.when(jnp.logical_not(at_low))
    def _():
        greet((dp - 4, tp))

    @pl.when(jnp.logical_not(at_high))
    def _():
        greet((dp + 4, tp))

    pl.semaphore_wait(barrier, 5 - jnp.where(at_end, 1, 0))

    def remote(source, place, send, recv, peer):
        return pltpu.make_async_remote_copy(
            src_ref=source, dst_ref=place, send_sem=send, recv_sem=recv,
            device_id=peer, device_id_type=MESH,
        )

    own_copies = [
        remote(
            hidden.at[:, columns_of(k, y)], tokens.at[k, mine, :],
            own_send.at[k], own_recv.at[k], x_peer,
        )
        for k in range(n_z)
    ]
    fwd_copies = [
        remote(
            tokens.at[k, mine_far, :], tokens.at[k, mine_far, :],
            fwd_send.at[k], fwd_recv.at[k], x_peer,
        )
        for k in range(n_z)
    ]
    ytok_copies = [
        remote(
            hidden.at[:, columns_of(k, 1 - y)], tokens.at[k, mine_far, :],
            ytok_send.at[k], ytok_recv.at[k], y_peer,
        )
        for k in range(n_z)
    ]
    ygrad_copies = [
        [
            remote(
                query_grad.at[:, pl.ds(n * chunk, chunk)],
                grads.at[far, pl.ds(n * chunk, chunk)],
                ygrad_send.at[n], ygrad_recv.at[n], y_peer,
            )
        ]
        for n in range(n_c - 1)
    ] + [
        [
            remote(
                source, grads.at[far, pl.ds(q_w + i * k_w, k_w)],
                ygrad_send.at[n_c - 1 + i], ygrad_recv.at[n_c - 1 + i], y_peer,
            )
            for i, source in enumerate((key_grad, value_grad))
        ]
    ]
    head_copies = [
        remote(
            head_out.at[j], head_in.at[j], head_send.at[j], head_recv.at[j], x_peer
        )
        for j in range(pieces)
    ]
    core_copies = [
        [
            remote(
                core_out.at[k, n], core_in.at[k, n],
                core_send.at[k, n], core_recv.at[k, n], core_peer,
            )
            for n in range(n_c)
        ]
        for k in range(n_z)
    ]
    z_copies = [
        [
            remote(
                z_out.at[k, n], z_in.at[down[k], target[k], n],
                z_send.at[k, n], z_recv.at[down[k], target[k], n],
                (dp + 4 - 8 * down[k], tp),
            )
            for n in range(n_c)
        ]
        for k in range(n_z - 1)
    ]

    own_copies[0].start()
    ytok_copies[0].start()
    own_copies[1].start()
    for n in range(n_c - 1):
        ygrad_copies[n][0].start()
    ytok_copies[1].start()
    for copy in ygrad_copies[n_c - 1]:
        copy.start()
    for copy in ytok_copies[2:]:
        copy.start()

    for copy in grad_loads + weight_loads:
        copy.wait()

    def head_piece(j):
        columns = pl.ds(j * width, width)
        head_out[j] = contract_cols(grads[theirs, :], weights[columns, :]).astype(bf16)
        own_head[:, columns] = contract_cols(grads[mine, :], weights[columns, :])

    def block(k, n, which):
        start = pl.multiple_of(which * rows, rows)
        return contract_rows(
            tokens[k, :, pl.ds(start, rows)], grads[:, pl.ds(n * chunk, chunk)]
        )

    def arrive(k):
        token_loads[k].wait()
        own_copies[k].wait_recv()
        fwd_copies[k].wait_recv()

    def partial(k, n):
        if k == 0:
            for copy in ygrad_copies[n]:
                copy.wait_recv()
        core_out[k, n] = block(k, n, 1 - core).astype(bf16)
        core_copies[k][n].start()
        total[k, n] = block(k, n, core)

    def pass_on(k, n, at_line_end):
        def run():
            core_copies[k][n].wait_recv()
            summed = total[k, n] + core_in[k, n].astype(f32)
            if not at_line_end:
                z_copies[k][n].wait_recv()
                summed = summed + z_in[down[k], target[k], n].astype(f32)
            z_out[k, n] = summed.astype(bf16)
            z_copies[k][n].start()

        pl.when(at_end if at_line_end else jnp.logical_not(at_end))(run)

    def from_line(direction, n):
        return remote(
            z_out.at[0, n], z_in.at[direction, z, n],
            z_send.at[0, n], z_recv.at[direction, z, n], x_peer,
        )

    def finish(n):
        last = n_z - 1
        span = pl.ds(n * chunk, chunk)
        core_copies[last][n].wait_recv()
        final[:, span] = total[last, n] + core_in[last, n].astype(f32)

        for direction, edge in ((0, at_low), (1, at_high)):
            @pl.when(jnp.logical_not(edge))
            def _():
                from_line(direction, n).wait_recv()
                final[:, span] += z_in[direction, z, n].astype(f32)

    def add_heads(j):
        head_copies[j].wait_recv()
        columns = pl.ds(j * width, width)
        own = own_head[:, columns]
        result[:, columns] = (own + head_in[j].astype(f32)).astype(result.dtype)

    chunks = range(n_c)
    ready = sent = 0

    def prepare(count):
        nonlocal ready
        for j in range(ready, min(ready + count, pieces)):
            head_piece(j)
        ready = min(ready + count, pieces)

    def send_heads(count):
        nonlocal sent
        for j in range(sent, min(sent + count, ready)):
            head_copies[j].start()
        sent = min(sent + count, ready)

    prepare(3)
    ytok_copies[0].wait_recv()
    fwd_copies[0].start()
    for copy in own_copies[2:]:
        copy.start()
    prepare(2)
    arrive(0)
    for n in chunks[:-1]:
        partial(0, n)
    for n in chunks[:-1]:
        pass_on(0, n, True)
    for k in range(1, n_z):
        ytok_copies[k].wait_recv()
        fwd_copies[k].start()
        send_heads(1 if k < n_z - 1 else pieces)
        if k == 1:
            partial(0, n_c - 1)
            pass_on(0, n_c - 1, True)
        prepare(1 if k < n_z - 1 else pieces)
        send_heads(0 if k < n_z - 1 else pieces)
        if k >= 2:
            arrive(k - 1)
            for n in chunks:
                partial(k - 1, n)
                if n > 0:
                    pass_on(k - 1, n - 1, True)
            pass_on(k - 1, n_c - 1, True)
            for n in chunks:
                pass_on(k - 2, n, False)
    arrive(n_z - 1)
    for n in chunks:
        partial(n_z - 1, n)
    for n in chunks:
        pass_on(n_z - 2, n, False)
    for n in chunks:
        finish(n)
    for j in range(pieces):
        add_heads(j)
    grad_sends = [copy for copies in ygrad_copies for copy in copies]
    flat = [copy for copies in core_copies + z_copies for copy in copies]
    for copy in own_copies + fwd_copies + ytok_copies + grad_sends + head_copies + flat:
        copy.wait_send()


def place(result, final, out_hidden, out_query, out_key, out_value, sem):
    q_w, k_w = out_query.shape[1], out_key.shape[1]
    copies = [
        pltpu.make_async_copy(result, out_hidden, sem.at[0]),
        pltpu.make_async_copy(final.at[:, pl.ds(0, q_w)], out_query, sem.at[1]),
        pltpu.make_async_copy(final.at[:, pl.ds(q_w, k_w)], out_key, sem.at[2]),
        pltpu.make_async_copy(
            final.at[:, pl.ds(q_w + k_w, k_w)], out_value, sem.at[3]
        ),
    ]
    for copy in copies:
        copy.start()
    for copy in copies:
        copy.wait()


def fused(n_dp, hidden, query_grad, key_grad, value_grad, w_query, w_key, w_value):
    half, depth = hidden.shape
    group = query_grad.shape[0]
    q_w, k_w = w_query.shape[1], w_key.shape[1]
    wide = q_w + 2 * k_w
    rows = depth // n_dp
    if q_w % (2 * k_w) or rows % 128 or k_w % 128 or half * 2 != group:
        return local(hidden, query_grad, key_grad, value_grad, w_query, w_key, w_value)
    n_z = n_dp // 4
    n_c = wide // (2 * k_w)
    chunk = 2 * k_w
    pieces = 2 * n_z
    width = depth // pieces
    bf16, f32 = jnp.bfloat16, jnp.float32
    dma = pltpu.SemaphoreType.DMA
    held = pl.pallas_call(
        functools.partial(kernel, n_z, pieces, n_c),
        out_shape=(pltpu.VMEM((half, depth), bf16), pltpu.VMEM((rows, wide), f32)),
        in_specs=[pl.BlockSpec(memory_space=pl.ANY)] * 7,
        out_specs=(pl.BlockSpec(memory_space=pltpu.VMEM),) * 2,
        scratch_shapes=[
            pltpu.VMEM((n_z, 2 * group, 2 * rows), bf16),
            pltpu.VMEM((2 * group, wide), bf16),
            pltpu.VMEM((depth, wide), bf16),
            pltpu.VMEM((pieces, half, width), bf16),
            pltpu.VMEM((pieces, half, width), bf16),
            pltpu.VMEM((n_z, n_c, rows, chunk), bf16),
            pltpu.VMEM((n_z, n_c, rows, chunk), bf16),
            pltpu.VMEM((n_z, n_c, rows, chunk), f32),
            pltpu.VMEM((n_z - 1, n_c, rows, chunk), bf16),
            pltpu.VMEM((2, n_z, n_c, rows, chunk), bf16),
            pltpu.VMEM((half, depth), f32),
            dma((6 + n_z,)),
            dma((n_z,)), dma((n_z,)),
            dma((n_z,)), dma((n_z,)),
            dma((n_z,)), dma((n_z,)),
            dma((n_c + 1,)), dma((n_c + 1,)),
            dma((pieces,)), dma((pieces,)),
            dma((n_z, n_c)), dma((n_z, n_c)),
            dma((n_z - 1, n_c)), dma((2, n_z, n_c)),
        ],
        compiler_params=pltpu.CompilerParams(
            collective_id=0, has_side_effects=True, vmem_limit_bytes=56 * 1024 * 1024
        ),
    )(hidden, query_grad, key_grad, value_grad, w_query, w_key, w_value)
    return pl.pallas_call(
        place,
        out_shape=(
            jax.ShapeDtypeStruct((half, depth), bf16),
            jax.ShapeDtypeStruct((rows, q_w), f32),
            jax.ShapeDtypeStruct((rows, k_w), f32),
            jax.ShapeDtypeStruct((rows, k_w), f32),
        ),
        in_specs=[pl.BlockSpec(memory_space=pltpu.VMEM)] * 2,
        out_specs=(pl.BlockSpec(memory_space=pl.ANY),) * 4,
        scratch_shapes=[dma((4,))],
    )(*[pltpu.with_memory_space_constraint(a, pltpu.VMEM) for a in held])


def solution(mesh):
    placed = (
        P(("dp", "tp"), None),
        P("dp", "tp"),
        P("dp", "tp"),
        P("dp", "tp"),
        P(None, "tp"),
        P(None, "tp"),
        P(None, "tp"),
    )
    n_dp, n_tp = mesh.shape["dp"], mesh.shape["tp"]
    body = local
    if n_tp == 2 and n_dp % 4 == 0 and n_dp > 8:
        body = functools.partial(fused, n_dp)
    return jax.shard_map(
        body,
        mesh=mesh,
        in_specs=placed,
        out_specs=(P(("dp", "tp"), None), P("dp", "tp"), P("dp", "tp"), P("dp", "tp")),
        check_vma=False,
    )
```

time: 56.7 us -> 53.6 us (0.945)
  Pallas kernels: 55.9 us -> 52.8 us
    pallas_call x1, Pallas kernels: 54.7 us -> 51.5 us  [fused(): pl.pallas_call(functools.partial(kernel, n_z, pieces, n_c), out_shape=(pl...]
where the time goes in v1:
time: 53.6 us; the launch traced here: 53.4 us
  Pallas kernels  52.8 us (99%)
  between operations  0.64 us (1%)
    pallas_call x1, Pallas kernels, fused(): pl.pallas_call(functools.partial(kernel, n_z, pieces, n_c), out_shape=(pl...  51.5 us
    pallas_call x1, Pallas kernels, fused(): pl.pallas_call(place, out_shape=(jax.ShapeDtypeStruct((half, depth), bf16...  1.25 us

profile of v1, /device:TPU:0, one launch (start us, length us, event | category | flops | bytes accessed | tf_op | source)
XLA Modules:
  0.0 53.4 jit_solution(3169371829484098866)
XLA Ops:
  0.6 51.5 %shard_map.102 = (bf16[128,4096]{1,0:T(8,128)(2,1)S(1)}, f32[256,768]{1,0:T(8,128)S(1)}) custom-call(bf16[128,4096]{1,0:T(8,128)(2,1)} %hidden.1, bf16[256,512]{1,0:T(8,128)(2,1)} %query_grad.1, bf16[256,128]{1,0:T(8,128)(2,1)} %key_grad.1, bf16[256,128]{1,0:T(8,128)(2,1)} %value_grad.1, bf16[4096,512]{1,0:T(8,128)(2,1)} %w_query.1, ...), custom_call_target="tpu_custom_call" | custom-call | tf_op jit(solution)/shard_map/pallas_call | solution.py:379
  52.2 1.3 %shard_map.103 = (bf16[128,4096]{1,0:T(8,128)(2,1)}, f32[256,512]{1,0:T(8,128)}, f32[256,128]{1,0:T(8,128)}, f32[256,128]{1,0:T(8,128)}) custom-call(bf16[128,4096]{1,0:T(8,128)(2,1)S(1)} %get-tuple-element.6.result, f32[256,768]{1,0:T(8,128)S(1)} %get-tuple-element.7.final), custom_call_target="tpu_custom_call" | custom-call | tf_op jit(solution)/shard_map/pallas_call | solution.py:409

commit v2 on v1

--- a/solution.py
+++ b/solution.py
@@ -63,9 +63,8 @@
     result, final,
     tokens, grads, weights, head_out, head_in, core_out, core_in,
     total, z_out, z_in, own_head,
-    load_sem, own_send, own_recv, fwd_send, fwd_recv, ytok_send, ytok_recv,
-    ygrad_send, ygrad_recv, head_send, head_recv, core_send, core_recv,
-    z_send, z_recv,
+    load_sem, send_sem, x_recv, ytok_recv, ygrad_recv, head_recv, core_recv, z_recv,
+    seen_sem, go_sem,
 ):
     dp = lax.axis_index("dp")
     tp = lax.axis_index("tp")
@@ -100,44 +99,40 @@
         return pl.ds(pl.multiple_of((target[k] * 2 + side) * pair, pair), pair)
 
     def load(index, source, place):
-        copy = pltpu.make_async_copy(source, place, load_sem.at[index])
-        copy.start()
-        return copy
+        pltpu.make_async_copy(source, place, load_sem.at[index]).start()
 
     near = pl.ds(0, group)
     far = pl.ds(group, group)
-    grad_loads = [
-        load(0, query_grad, grads.at[near, pl.ds(0, q_w)]),
-        load(1, key_grad, grads.at[near, pl.ds(q_w, k_w)]),
-        load(2, value_grad, grads.at[near, pl.ds(q_w + k_w, k_w)]),
-    ]
-    weight_loads = [
-        load(3, w_query, weights.at[:, pl.ds(0, q_w)]),
-        load(4, w_key, weights.at[:, pl.ds(q_w, k_w)]),
-        load(5, w_value, weights.at[:, pl.ds(q_w + k_w, k_w)]),
-    ]
-    token_loads = [
-        load(6 + k, hidden.at[:, columns_of(k, y)], tokens.at[k, mine, :])
-        for k in range(n_z)
-    ]
+    load(0, query_grad, grads.at[near, pl.ds(0, q_w)])
+    load(0, key_grad, grads.at[near, pl.ds(q_w, k_w)])
+    load(0, value_grad, grads.at[near, pl.ds(q_w + k_w, k_w)])
+    load(1, w_query, weights.at[:, pl.ds(0, q_w)])
+    load(1, w_key, weights.at[:, pl.ds(q_w, k_w)])
+    load(1, w_value, weights.at[:, pl.ds(q_w + k_w, k_w)])
+    for k in range(n_z):
+        load(2, hidden.at[:, columns_of(k, y)], tokens.at[k, mine, :])
 
     barrier = pltpu.get_barrier_semaphore()
 
     def greet(peer):
         pl.semaphore_signal(barrier, inc=1, device_id=peer, device_id_type=MESH)
 
-    for peer in (x_peer, y_peer, core_peer):
-        greet(peer)
-
-    @pl.when(jnp.logical_not(at_low))
-    def _():
-        greet((dp - 4, tp))
-
-    @pl.when(jnp.logical_not(at_high))
-    def _():
-        greet((dp + 4, tp))
-
-    pl.semaphore_wait(barrier, 5 - jnp.where(at_end, 1, 0))
+    greet(x_peer)
+    greet(core_peer)
+    scout = core == 0
+    low_peer, high_peer = (dp - 4, tp), (dp + 4, tp)
+    around = 3 - jnp.where(at_end, 1, 0)
+
+    def around_line(tell):
+        tell(y_peer)
+        pl.when(jnp.logical_not(at_low))(lambda: tell(low_peer))
+        pl.when(jnp.logical_not(at_high))(lambda: tell(high_peer))
+
+    pl.when(scout)(lambda: around_line(greet))
+    pl.semaphore_wait(barrier, 2 + jnp.where(scout, around, 0))
+
+    def notify(semaphore, peer):
+        pl.semaphore_signal(semaphore, inc=1, device_id=peer, device_id_type=MESH)
 
     def remote(source, place, send, recv, peer):
         return pltpu.make_async_remote_copy(
@@ -148,45 +143,38 @@
     own_copies = [
         remote(
             hidden.at[:, columns_of(k, y)], tokens.at[k, mine, :],
-            own_send.at[k], own_recv.at[k], x_peer,
+            send_sem.at[0], x_recv.at[k], x_peer,
         )
         for k in range(n_z)
     ]
     fwd_copies = [
         remote(
             tokens.at[k, mine_far, :], tokens.at[k, mine_far, :],
-            fwd_send.at[k], fwd_recv.at[k], x_peer,
+            send_sem.at[1], x_recv.at[k], x_peer,
         )
         for k in range(n_z)
     ]
     ytok_copies = [
         remote(
             hidden.at[:, columns_of(k, 1 - y)], tokens.at[k, mine_far, :],
-            ytok_send.at[k], ytok_recv.at[k], y_peer,
+            send_sem.at[2], ytok_recv.at[k], y_peer,
         )
         for k in range(n_z)
     ]
+
+    def ygrad(source, first, n):
+        span = pl.ds(first, source.shape[1])
+        return remote(
+            source, grads.at[far, span], send_sem.at[3], ygrad_recv.at[n], y_peer
+        )
+
     ygrad_copies = [
-        [
-            remote(
-                query_grad.at[:, pl.ds(n * chunk, chunk)],
-                grads.at[far, pl.ds(n * chunk, chunk)],
-                ygrad_send.at[n], ygrad_recv.at[n], y_peer,
-            )
-        ]
+        [ygrad(query_grad.at[:, pl.ds(n * chunk, chunk)], n * chunk, n)]
         for n in range(n_c - 1)
-    ] + [
-        [
-            remote(
-                source, grads.at[far, pl.ds(q_w + i * k_w, k_w)],
-                ygrad_send.at[n_c - 1 + i], ygrad_recv.at[n_c - 1 + i], y_peer,
-            )
-            for i, source in enumerate((key_grad, value_grad))
-        ]
-    ]
+    ] + [[ygrad(key_grad, q_w, n_c - 1), ygrad(value_grad, q_w + k_w, n_c - 1)]]
     head_copies = [
         remote(
-            head_out.at[j], head_in.at[j], head_send.at[j], head_recv.at[j], x_peer
+            head_out.at[j], head_in.at[j], send_sem.at[4], head_recv.at[j], x_peer
         )
         for j in range(pieces)
     ]
@@ -194,17 +182,27 @@
         [
             remote(
                 core_out.at[k, n], core_in.at[k, n],
-                core_send.at[k, n], core_recv.at[k, n], core_peer,
+                send_sem.at[5], core_recv.at[n if k == 0 else n_c + k - 1], core_peer,
             )
             for n in range(n_c)
         ]
         for k in range(n_z)
     ]
+    def place_on(step, below):
+        i = below + 1 if order[below][step] > below else below - 1
+        if not 0 <= i < n_z or order[below][step] == below:
+            return 0
+        to = order[below][step]
+        if to == i:
+            return n_z - 1 if below < i else n_z
+        return order[i].index(to)
+
+    z_slot = [pick([place_on(k, i) for i in range(n_z)], z) for k in range(n_z - 1)]
     z_copies = [
         [
             remote(
-                z_out.at[k, n], z_in.at[down[k], target[k], n],
-                z_send.at[k, n], z_recv.at[down[k], target[k], n],
+                z_out.at[k, n], z_in.at[z_slot[k], n],
+                send_sem.at[6], z_recv.at[z_slot[k], n],
                 (dp + 4 - 8 * down[k], tp),
             )
             for n in range(n_c)
@@ -212,19 +210,39 @@
         for k in range(n_z - 1)
     ]
 
-    own_copies[0].start()
-    ytok_copies[0].start()
-    own_copies[1].start()
-    for n in range(n_c - 1):
-        ygrad_copies[n][0].start()
-    ytok_copies[1].start()
-    for copy in ygrad_copies[n_c - 1]:
+    def landed(whole, semaphore):
+        pltpu.make_async_copy(whole, whole, semaphore).wait()
+
+    for copy in own_copies[:3]:
         copy.start()
-    for copy in ytok_copies[2:]:
-        copy.start()
-
-    for copy in grad_loads + weight_loads:
-        copy.wait()
+
+    def start_y():
+        ytok_copies[0].start()
+        for n in range(n_c - 1):
+            ygrad_copies[n][0].start()
+        ytok_copies[1].start()
+        for copy in ygrad_copies[n_c - 1]:
+            copy.start()
+        for copy in ytok_copies[2:]:
+            copy.start()
+
+    @pl.when(scout)
+    def _():
+        start_y()
+        around_line(lambda peer: notify(seen_sem, peer))
+        pl.semaphore_wait(seen_sem, around)
+        notify(go_sem, core_peer)
+
+    @pl.when(jnp.logical_not(scout))
+    def _():
+        pl.semaphore_wait(go_sem, 1)
+        start_y()
+
+    def loaded(index, whole):
+        pltpu.make_async_copy(whole, whole, load_sem.at[index]).wait()
+
+    loaded(0, grads.at[near, :])
+    loaded(1, weights)
 
     def head_piece(j):
         columns = pl.ds(j * width, width)
@@ -238,47 +256,45 @@
         )
 
     def arrive(k):
-        token_loads[k].wait()
-        own_copies[k].wait_recv()
-        fwd_copies[k].wait_recv()
+        if k == 0:
+            loaded(2, tokens.at[:, mine, :])
+        landed(tokens.at[k, pl.ds(0, group), :], x_recv.at[k])
 
     def partial(k, n):
         if k == 0:
-            for copy in ygrad_copies[n]:
-                copy.wait_recv()
+            landed(grads.at[far, pl.ds(n * chunk, chunk)], ygrad_recv.at[n])
         core_out[k, n] = block(k, n, 1 - core).astype(bf16)
         core_copies[k][n].start()
         total[k, n] = block(k, n, core)
 
+    def sibling_part(k, n):
+        if k == 0:
+            landed(core_in.at[k, n], core_recv.at[n])
+        elif n == 0:
+            landed(core_in.at[k], core_recv.at[n_c + k - 1])
+        return core_in[k, n].astype(f32)
+
     def pass_on(k, n, at_line_end):
         def run():
-            core_copies[k][n].wait_recv()
-            summed = total[k, n] + core_in[k, n].astype(f32)
+            summed = total[k, n] + sibling_part(k, n)
             if not at_line_end:
-                z_copies[k][n].wait_recv()
-                summed = summed + z_in[down[k], target[k], n].astype(f32)
+                landed(z_in.at[k, n], z_recv.at[k, n])
+                summed = summed + z_in[k, n].astype(f32)
             z_out[k, n] = summed.astype(bf16)
             z_copies[k][n].start()
 
         pl.when(at_end if at_line_end else jnp.logical_not(at_end))(run)
-
-    def from_line(direction, n):
-        return remote(
-            z_out.at[0, n], z_in.at[direction, z, n],
-            z_send.at[0, n], z_recv.at[direction, z, n], x_peer,
-        )
 
     def finish(n):
         last = n_z - 1
         span = pl.ds(n * chunk, chunk)
-        core_copies[last][n].wait_recv()
-        final[:, span] = total[last, n] + core_in[last, n].astype(f32)
-
-        for direction, edge in ((0, at_low), (1, at_high)):
+        final[:, span] = total[last, n] + sibling_part(last, n)
+
+        for slot, edge in ((n_z - 1, at_low), (n_z, at_high)):
             @pl.when(jnp.logical_not(edge))
             def _():
-                from_line(direction, n).wait_recv()
-                final[:, span] += z_in[direction, z, n].astype(f32)
+                landed(z_in.at[slot, n], z_recv.at[slot, n])
+                final[:, span] += z_in[slot, n].astype(f32)
 
     def add_heads(j):
         head_copies[j].wait_recv()
@@ -304,8 +320,9 @@
     prepare(3)
     ytok_copies[0].wait_recv()
     fwd_copies[0].start()
-    for copy in own_copies[2:]:
+    for copy in own_copies[3:]:
         copy.start()
+    send_heads(1)
     prepare(2)
     arrive(0)
     for n in chunks[:-1]:
@@ -325,9 +342,8 @@
             arrive(k - 1)
             for n in chunks:
                 partial(k - 1, n)
-                if n > 0:
-                    pass_on(k - 1, n - 1, True)
-            pass_on(k - 1, n_c - 1, True)
+            for n in chunks:
+                pass_on(k - 1, n, True)
             for n in chunks:
                 pass_on(k - 2, n, False)
     arrive(n_z - 1)
@@ -339,10 +355,12 @@
         finish(n)
     for j in range(pieces):
         add_heads(j)
-    grad_sends = [copy for copies in ygrad_copies for copy in copies]
-    flat = [copy for copies in core_copies + z_copies for copy in copies]
-    for copy in own_copies + fwd_copies + ytok_copies + grad_sends + head_copies + flat:
-        copy.wait_send()
+    sources = (
+        tokens.at[:, mine, :], tokens.at[:, mine, :], tokens.at[:, mine, :],
+        grads.at[near, :], head_out, core_out, z_out,
+    )
+    for i, source in enumerate(sources):
+        landed(source, send_sem.at[i])
 
 
 def place(result, final, out_hidden, out_query, out_key, out_value, sem):
@@ -391,16 +409,11 @@
             pltpu.VMEM((n_z, n_c, rows, chunk), bf16),
             pltpu.VMEM((n_z, n_c, rows, chunk), f32),
             pltpu.VMEM((n_z - 1, n_c, rows, chunk), bf16),
-            pltpu.VMEM((2, n_z, n_c, rows, chunk), bf16),
+            pltpu.VMEM((n_z + 1, n_c, rows, chunk), bf16),
             pltpu.VMEM((half, depth), f32),
-            dma((6 + n_z,)),
-            dma((n_z,)), dma((n_z,)),
-            dma((n_z,)), dma((n_z,)),
-            dma((n_z,)), dma((n_z,)),
-            dma((n_c + 1,)), dma((n_c + 1,)),
-            dma((pieces,)), dma((pieces,)),
-            dma((n_z, n_c)), dma((n_z, n_c)),
-            dma((n_z - 1, n_c)), dma((2, n_z, n_c)),
+            dma((3,)), dma((7,)), dma((n_z,)), dma((n_z,)), dma((n_c,)), dma((pieces,)),
+            dma((n_c + n_z - 1,)), dma((n_z + 1, n_c)),
+            pltpu.SemaphoreType.REGULAR, pltpu.SemaphoreType.REGULAR,
         ],
         compiler_params=pltpu.CompilerParams(
             collective_id=0, has_side_effects=True, vmem_limit_bytes=56 * 1024 * 1024

time: 53.6 us -> 52.1 us (0.972)
  Pallas kernels: 52.8 us -> 51.3 us
    pallas_call x1, Pallas kernels: 51.5 us -> 50 us  [fused(): pl.pallas_call(functools.partial(kernel, n_z, pieces, n_c), out_shape=(pl...]
where the time goes in v2:
time: 52.1 us; the launch traced here: 51.9 us
  Pallas kernels  51.3 us (98%)
  between operations  0.64 us (1%)
    pallas_call x1, Pallas kernels, fused(): pl.pallas_call(functools.partial(kernel, n_z, pieces, n_c), out_shape=(pl...  50 us
    pallas_call x1, Pallas kernels, fused(): pl.pallas_call(place, out_shape=(jax.ShapeDtypeStruct((half, depth), bf16...  1.25 us

profile of v2, /device:TPU:0, one launch (start us, length us, event | category | flops | bytes accessed | tf_op | source)
XLA Modules:
  0.0 51.9 jit_solution(15653210214481832407)
XLA Ops:
  0.6 50.0 %shard_map.102 = (bf16[128,4096]{1,0:T(8,128)(2,1)S(1)}, f32[256,768]{1,0:T(8,128)S(1)}) custom-call(bf16[128,4096]{1,0:T(8,128)(2,1)} %hidden.1, bf16[256,512]{1,0:T(8,128)(2,1)} %query_grad.1, bf16[256,128]{1,0:T(8,128)(2,1)} %key_grad.1, bf16[256,128]{1,0:T(8,128)(2,1)} %value_grad.1, bf16[4096,512]{1,0:T(8,128)(2,1)} %w_query.1, ...), custom_call_target="tpu_custom_call" | custom-call | tf_op jit(solution)/shard_map/pallas_call | solution.py:397
  50.7 1.3 %shard_map.103 = (bf16[128,4096]{1,0:T(8,128)(2,1)}, f32[256,512]{1,0:T(8,128)}, f32[256,128]{1,0:T(8,128)}, f32[256,128]{1,0:T(8,128)}) custom-call(bf16[128,4096]{1,0:T(8,128)(2,1)S(1)} %get-tuple-element.6.result, f32[256,768]{1,0:T(8,128)S(1)} %get-tuple-element.7.final), custom_call_target="tpu_custom_call" | custom-call | tf_op jit(solution)/shard_map/pallas_call | solution.py:422

commit v3 on v2

--- a/solution.py
+++ b/solution.py
@@ -62,9 +62,9 @@
     hidden, query_grad, key_grad, value_grad, w_query, w_key, w_value,
     result, final,
     tokens, grads, weights, head_out, head_in, core_out, core_in,
-    total, z_out, z_in, own_head,
+    total, z_out, z_in, own_head, gathered, own_grads,
     load_sem, send_sem, x_recv, ytok_recv, ygrad_recv, head_recv, core_recv, z_recv,
-    seen_sem, go_sem,
+    unit_send, unit_recv, plane_recv, seen_sem, go_sem,
 ):
     dp = lax.axis_index("dp")
     tp = lax.axis_index("tp")
@@ -77,7 +77,9 @@
     k_w = key_grad.shape[1]
     rows = final.shape[0]
     pair = 2 * rows
-    width = hidden.shape[1] // pieces
+    width = hidden.shape[1] // 2 // pieces
+    own_first = hidden.shape[1] // 2
+    unit = rows // 2
     chunk = 2 * k_w
     bf16, f32 = jnp.bfloat16, jnp.float32
 
@@ -210,19 +212,54 @@
         for k in range(n_z - 1)
     ]
 
+    def units(source):
+        return pl.ds(pl.multiple_of(source * unit, unit), unit)
+
+    fetches = [
+        remote(
+            source.at[units(dp), :],
+            gathered.at[units(dp), pl.ds(first, source.shape[1])],
+            send_sem.at[7], plane_recv.at[0], x_peer,
+        )
+        for source, first in ((w_query, 0), (w_key, q_w), (w_value, q_w + k_w))
+    ]
+    lend_grads = remote(
+        grads.at[theirs, :], own_grads, send_sem.at[8], plane_recv.at[1], x_peer
+    )
+
+    def unit_copy(direction, s):
+        rows_of = units(dp - 4 * s if direction == 0 else dp + 4 * s)
+        return remote(
+            gathered.at[rows_of, :], gathered.at[rows_of, :],
+            unit_send.at[direction, s], unit_recv.at[direction, s],
+            high_peer if direction == 0 else low_peer,
+        )
+
+    def to_sibling(source, across):
+        remote(
+            gathered.at[units(source), :], gathered.at[units(source), :],
+            send_sem.at[10], plane_recv.at[3 + across], core_peer,
+        ).start()
+
+    def to_plane(source):
+        remote(
+            gathered.at[units(source), :], gathered.at[units(source), :],
+            send_sem.at[9], plane_recv.at[2], y_peer,
+        ).start()
+        to_sibling(source, 0)
+
     def landed(whole, semaphore):
         pltpu.make_async_copy(whole, whole, semaphore).wait()
 
-    for copy in own_copies[:3]:
+    for copy in own_copies[:1] + fetches:
         copy.start()
 
     def start_y():
-        ytok_copies[0].start()
-        for n in range(n_c - 1):
-            ygrad_copies[n][0].start()
-        ytok_copies[1].start()
-        for copy in ygrad_copies[n_c - 1]:
+        for copy in ytok_copies[:2]:
             copy.start()
+        for copies in ygrad_copies:
+            for copy in copies:
+                copy.start()
         for copy in ytok_copies[2:]:
             copy.start()
 
@@ -245,8 +282,10 @@
     loaded(1, weights)
 
     def head_piece(j):
+        columns = pl.ds(own_first + j * width, width)
+        head_out[j] = contract_cols(grads[theirs, :], weights[columns, :]).astype(bf16)
+        own_head[:, columns] = contract_cols(grads[mine, :], weights[columns, :])
         columns = pl.ds(j * width, width)
-        head_out[j] = contract_cols(grads[theirs, :], weights[columns, :]).astype(bf16)
         own_head[:, columns] = contract_cols(grads[mine, :], weights[columns, :])
 
     def block(k, n, which):
@@ -286,7 +325,6 @@
         pl.when(at_end if at_line_end else jnp.logical_not(at_end))(run)
 
     def finish(n):
-        last = n_z - 1
         span = pl.ds(n * chunk, chunk)
         final[:, span] = total[last, n] + sibling_part(last, n)
 
@@ -298,9 +336,30 @@
 
     def add_heads(j):
         head_copies[j].wait_recv()
-        columns = pl.ds(j * width, width)
+        columns = pl.ds(own_first + j * width, width)
         own = own_head[:, columns]
         result[:, columns] = (own + head_in[j].astype(f32)).astype(result.dtype)
+
+    def add_gathered(i, side):
+        start = pl.multiple_of((i * 4 + side * 2) * unit, 2 * unit)
+        columns = pl.ds(start, 2 * unit)
+        other = contract_cols(own_grads[...], gathered[columns, :])
+        result[:, columns] = (own_head[:, columns] + other).astype(result.dtype)
+
+    def relay(s):
+        for direction, exists, onward, step in (
+            (0, z >= s, jnp.logical_not(at_high), -4),
+            (1, z <= n_z - 1 - s, jnp.logical_not(at_low), 4),
+        ):
+            @pl.when(exists)
+            def _():
+                spread(direction, s, onward, dp + step * s)
+
+    def spread(direction, s, onward, source):
+        landed(gathered.at[units(source), :], unit_recv.at[direction, s - 1])
+        if s < n_z - 1:
+            pl.when(onward)(unit_copy(direction, s).start)
+        to_plane(source)
 
     chunks = range(n_c)
     ready = sent = 0
@@ -317,47 +376,78 @@
             head_copies[j].start()
         sent = min(sent + count, ready)
 
-    prepare(3)
-    ytok_copies[0].wait_recv()
-    fwd_copies[0].start()
-    for copy in own_copies[3:]:
-        copy.start()
-    send_heads(1)
-    prepare(2)
-    arrive(0)
-    for n in chunks[:-1]:
-        partial(0, n)
-    for n in chunks[:-1]:
-        pass_on(0, n, True)
-    for k in range(1, n_z):
+    last = n_z - 1
+    in_plane = n_z * unit
+
+    def forward_tokens(k):
         ytok_copies[k].wait_recv()
         fwd_copies[k].start()
-        send_heads(1 if k < n_z - 1 else pieces)
-        if k == 1:
-            partial(0, n_c - 1)
-            pass_on(0, n_c - 1, True)
-        prepare(1 if k < n_z - 1 else pieces)
-        send_heads(0 if k < n_z - 1 else pieces)
-        if k >= 2:
-            arrive(k - 1)
-            for n in chunks:
-                partial(k - 1, n)
-            for n in chunks:
-                pass_on(k - 1, n, True)
-            for n in chunks:
-                pass_on(k - 2, n, False)
-    arrive(n_z - 1)
+        if k < last:
+            own_copies[k + 1].start()
+
+    prepare(2)
+    forward_tokens(0)
+    prepare(1)
+    forward_tokens(1)
+    lend_grads.start()
+    landed(gathered.at[units(dp), :], plane_recv.at[0])
+    pl.when(jnp.logical_not(at_high))(unit_copy(0, 0).start)
+    pl.when(jnp.logical_not(at_low))(unit_copy(1, 0).start)
+    to_plane(dp)
+    prepare(pieces)
+    arrive(0)
     for n in chunks:
-        partial(n_z - 1, n)
+        partial(0, n)
+        pass_on(0, n, True)
+    relay(1)
+    for k in range(1, last):
+        forward_tokens(k + 1)
+        if k + 1 == last:
+            send_heads(pieces)
+        arrive(k)
+        for n in chunks:
+            partial(k, n)
+        for n in chunks:
+            pass_on(k, n, True)
+        for n in chunks:
+            pass_on(k - 1, n, False)
+        if k + 1 < last:
+            relay(k + 1)
     for n in chunks:
-        pass_on(n_z - 2, n, False)
+        pass_on(last - 1, n, False)
+    relay(last)
+    arrive(last)
     for n in chunks:
+        partial(last, n)
+    landed(own_grads, plane_recv.at[1])
+    landed(gathered.at[pl.ds(0, in_plane), :], plane_recv.at[3])
+    for i in range(n_z):
+        add_gathered(i, y)
+    for n in chunks[:-1]:
         finish(n)
+    landed(gathered.at[pl.ds(0, in_plane), :], plane_recv.at[2])
+    for i in range(n_z):
+        to_sibling(i * 4 + (1 - y) * 2 + core, 1)
+    finish(n_c - 1)
+    landed(gathered.at[pl.ds(0, in_plane), :], plane_recv.at[4])
+    for i in range(n_z):
+        add_gathered(i, 1 - y)
     for j in range(pieces):
         add_heads(j)
+    for s in range(n_z - 1):
+        for direction, sent_on in (
+            (0, jnp.logical_and(z >= s, jnp.logical_not(at_high))),
+            (1, jnp.logical_and(z <= n_z - 1 - s, jnp.logical_not(at_low))),
+        ):
+            @pl.when(sent_on)
+            def _():
+                landed(gathered.at[units(dp), :], unit_send.at[direction, s])
+
     sources = (
         tokens.at[:, mine, :], tokens.at[:, mine, :], tokens.at[:, mine, :],
         grads.at[near, :], head_out, core_out, z_out,
+        gathered.at[units(dp), :], own_grads, gathered.at[pl.ds(0, n_z * unit), :],
+        gathered.at[pl.ds(0, 2 * n_z * unit), :],
     )
     for i, source in enumerate(sources):
         landed(source, send_sem.at[i])
@@ -385,13 +475,13 @@
     q_w, k_w = w_query.shape[1], w_key.shape[1]
     wide = q_w + 2 * k_w
     rows = depth // n_dp
-    if q_w % (2 * k_w) or rows % 128 or k_w % 128 or half * 2 != group:
+    if q_w % (2 * k_w) or rows % 256 or k_w % 128 or half * 2 != group:
         return local(hidden, query_grad, key_grad, value_grad, w_query, w_key, w_value)
     n_z = n_dp // 4
     n_c = wide // (2 * k_w)
     chunk = 2 * k_w
-    pieces = 2 * n_z
-    width = depth // pieces
+    pieces = n_z
+    width = depth // 2 // pieces
     bf16, f32 = jnp.bfloat16, jnp.float32
     dma = pltpu.SemaphoreType.DMA
     held = pl.pallas_call(
@@ -411,8 +501,11 @@
             pltpu.VMEM((n_z - 1, n_c, rows, chunk), bf16),
             pltpu.VMEM((n_z + 1, n_c, rows, chunk), bf16),
             pltpu.VMEM((half, depth), f32),
-            dma((3,)), dma((7,)), dma((n_z,)), dma((n_z,)), dma((n_c,)), dma((pieces,)),
+            pltpu.VMEM((depth // 2, wide), bf16),
+            pltpu.VMEM((half, wide), bf16),
+            dma((3,)), dma((11,)), dma((n_z,)), dma((n_z,)), dma((n_c,)), dma((pieces,)),
             dma((n_c + n_z - 1,)), dma((n_z + 1, n_c)),
+            dma((2, n_z - 1)), dma((2, n_z - 1)), dma((5,)),
             pltpu.SemaphoreType.REGULAR, pltpu.SemaphoreType.REGULAR,
         ],
         compiler_params=pltpu.CompilerParams(

time: 52.1 us -> 48.8 us (0.937)
  Pallas kernels: 51.3 us -> 47.8 us
    pallas_call x1, Pallas kernels: 50 us -> 46.5 us  [fused(): pl.pallas_call(functools.partial(kernel, n_z, pieces, n_c), out_shape=(pl...]
where the time goes in v3:
time: 48.8 us; the launch traced here: 48.4 us
  Pallas kernels  47.8 us (98%)
  between operations  0.64 us (1%)
    pallas_call x1, Pallas kernels, fused(): pl.pallas_call(functools.partial(kernel, n_z, pieces, n_c), out_shape=(pl...  46.5 us
    pallas_call x1, Pallas kernels, fused(): pl.pallas_call(place, out_shape=(jax.ShapeDtypeStruct((half, depth), bf16...  1.25 us

profile of v3, /device:TPU:0, one launch (start us, length us, event | category | flops | bytes accessed | tf_op | source)
XLA Modules:
  0.0 48.4 jit_solution(17131303120904128006)
XLA Ops:
  0.6 46.5 %shard_map.102 = (bf16[128,4096]{1,0:T(8,128)(2,1)S(1)}, f32[256,768]{1,0:T(8,128)S(1)}) custom-call(bf16[128,4096]{1,0:T(8,128)(2,1)} %hidden.1, bf16[256,512]{1,0:T(8,128)(2,1)} %query_grad.1, bf16[256,128]{1,0:T(8,128)(2,1)} %key_grad.1, bf16[256,128]{1,0:T(8,128)(2,1)} %value_grad.1, bf16[4096,512]{1,0:T(8,128)(2,1)} %w_query.1, ...), custom_call_target="tpu_custom_call" | custom-call | tf_op jit(solution)/shard_map/pallas_call | solution.py:487
  47.2 1.3 %shard_map.103 = (bf16[128,4096]{1,0:T(8,128)(2,1)}, f32[256,512]{1,0:T(8,128)}, f32[256,128]{1,0:T(8,128)}, f32[256,128]{1,0:T(8,128)}) custom-call(bf16[128,4096]{1,0:T(8,128)(2,1)S(1)} %get-tuple-element.6.result, f32[256,768]{1,0:T(8,128)S(1)} %get-tuple-element.7.final), custom_call_target="tpu_custom_call" | custom-call | tf_op jit(solution)/shard_map/pallas_call | solution.py:515

commit v4 on v3

--- a/solution.py
+++ b/solution.py
@@ -64,7 +64,7 @@
     tokens, grads, weights, head_out, head_in, core_out, core_in,
     total, z_out, z_in, own_head, gathered, own_grads,
     load_sem, send_sem, x_recv, ytok_recv, ygrad_recv, head_recv, core_recv, z_recv,
-    unit_send, unit_recv, plane_recv, seen_sem, go_sem,
+    unit_send, unit_recv, plane_recv, across_recv, seen_sem, go_sem,
 ):
     dp = lax.axis_index("dp")
     tp = lax.axis_index("tp")
@@ -105,6 +105,24 @@
 
     near = pl.ds(0, group)
     far = pl.ds(group, group)
+
+    barrier = pltpu.get_barrier_semaphore()
+
+    def greet(peer):
+        pl.semaphore_signal(barrier, inc=1, device_id=peer, device_id_type=MESH)
+
+    greet(x_peer)
+    scout = core == 0
+    low_peer, high_peer = (dp - 4, tp), (dp + 4, tp)
+    around = 3 - jnp.where(at_end, 1, 0)
+
+    def around_line(tell):
+        tell(y_peer)
+        pl.when(jnp.logical_not(at_low))(lambda: tell(low_peer))
+        pl.when(jnp.logical_not(at_high))(lambda: tell(high_peer))
+
+    pl.when(scout)(lambda: around_line(greet))
+    pl.when(jnp.logical_not(scout))(lambda: greet(core_peer))
     load(0, query_grad, grads.at[near, pl.ds(0, q_w)])
     load(0, key_grad, grads.at[near, pl.ds(q_w, k_w)])
     load(0, value_grad, grads.at[near, pl.ds(q_w + k_w, k_w)])
@@ -114,24 +132,7 @@
     for k in range(n_z):
         load(2, hidden.at[:, columns_of(k, y)], tokens.at[k, mine, :])
 
-    barrier = pltpu.get_barrier_semaphore()
-
-    def greet(peer):
-        pl.semaphore_signal(barrier, inc=1, device_id=peer, device_id_type=MESH)
-
-    greet(x_peer)
-    greet(core_peer)
-    scout = core == 0
-    low_peer, high_peer = (dp - 4, tp), (dp + 4, tp)
-    around = 3 - jnp.where(at_end, 1, 0)
-
-    def around_line(tell):
-        tell(y_peer)
-        pl.when(jnp.logical_not(at_low))(lambda: tell(low_peer))
-        pl.when(jnp.logical_not(at_high))(lambda: tell(high_peer))
-
-    pl.when(scout)(lambda: around_line(greet))
-    pl.semaphore_wait(barrier, 2 + jnp.where(scout, around, 0))
+    pl.semaphore_wait(barrier, 1 + jnp.where(scout, 1 + around, 0))
 
     def notify(semaphore, peer):
         pl.semaphore_signal(semaphore, inc=1, device_id=peer, device_id_type=MESH)
@@ -238,34 +239,35 @@
     def to_sibling(source, across):
         remote(
             gathered.at[units(source), :], gathered.at[units(source), :],
-            send_sem.at[10], plane_recv.at[3 + across], core_peer,
+            send_sem.at[10], plane_recv.at[2 + across], core_peer,
         ).start()
 
     def to_plane(source):
         remote(
             gathered.at[units(source), :], gathered.at[units(source), :],
-            send_sem.at[9], plane_recv.at[2], y_peer,
+            send_sem.at[9], across_recv.at[source // 4], y_peer,
         ).start()
         to_sibling(source, 0)
 
     def landed(whole, semaphore):
         pltpu.make_async_copy(whole, whole, semaphore).wait()
 
+    def loaded(index, whole):
+        pltpu.make_async_copy(whole, whole, load_sem.at[index]).wait()
+
     for copy in own_copies[:1] + fetches:
         copy.start()
 
-    def start_y():
-        for copy in ytok_copies[:2]:
-            copy.start()
-        for copies in ygrad_copies:
-            for copy in copies:
-                copy.start()
-        for copy in ytok_copies[2:]:
+    def start_later_y():
+        later = ygrad_copies[0] + ytok_copies[1:2]
+        for copies in ygrad_copies[1:]:
+            later = later + copies
+        for copy in later + ytok_copies[2:]:
             copy.start()
 
     @pl.when(scout)
     def _():
-        start_y()
+        ytok_copies[0].start()
         around_line(lambda peer: notify(seen_sem, peer))
         pl.semaphore_wait(seen_sem, around)
         notify(go_sem, core_peer)
@@ -273,10 +275,8 @@
     @pl.when(jnp.logical_not(scout))
     def _():
         pl.semaphore_wait(go_sem, 1)
-        start_y()
-
-    def loaded(index, whole):
-        pltpu.make_async_copy(whole, whole, load_sem.at[index]).wait()
+        ytok_copies[0].start()
+        start_later_y()
 
     loaded(0, grads.at[near, :])
     loaded(1, weights)
@@ -382,54 +382,64 @@
     def forward_tokens(k):
         ytok_copies[k].wait_recv()
         fwd_copies[k].start()
-        if k < last:
-            own_copies[k + 1].start()
-
-    prepare(2)
+        for copy in own_copies[1:3] if k == 0 else own_copies[k + 1 : k + 2]:
+            if k != 1:
+                copy.start()
+        if k == 1:
+            lend_grads.start()
+        if k == last:
+            send_heads(pieces)
+
+    prepare(1)
+    pl.when(scout)(start_later_y)
+    prepare(1)
     forward_tokens(0)
     prepare(1)
-    forward_tokens(1)
-    lend_grads.start()
     landed(gathered.at[units(dp), :], plane_recv.at[0])
     pl.when(jnp.logical_not(at_high))(unit_copy(0, 0).start)
     pl.when(jnp.logical_not(at_low))(unit_copy(1, 0).start)
     to_plane(dp)
     prepare(pieces)
     arrive(0)
-    for n in chunks:
+    partial(0, 0)
+    forward_tokens(1)
+    pass_on(0, 0, True)
+    for n in chunks[1:]:
+        if n == n_c - 1:
+            relay(1)
         partial(0, n)
         pass_on(0, n, True)
-    relay(1)
+    pass_on(0, 0, False)
     for k in range(1, last):
         forward_tokens(k + 1)
-        if k + 1 == last:
-            send_heads(pieces)
         arrive(k)
         for n in chunks:
             partial(k, n)
         for n in chunks:
             pass_on(k, n, True)
-        for n in chunks:
+        for n in chunks[1:]:
             pass_on(k - 1, n, False)
+        pass_on(k, 0, False)
         if k + 1 < last:
             relay(k + 1)
-    for n in chunks:
+    for n in chunks[1:]:
         pass_on(last - 1, n, False)
     relay(last)
     arrive(last)
     for n in chunks:
         partial(last, n)
     landed(own_grads, plane_recv.at[1])
-    landed(gathered.at[pl.ds(0, in_plane), :], plane_recv.at[3])
+    landed(gathered.at[pl.ds(0, in_plane), :], plane_recv.at[2])
     for i in range(n_z):
         add_gathered(i, y)
     for n in chunks[:-1]:
         finish(n)
-    landed(gathered.at[pl.ds(0, in_plane), :], plane_recv.at[2])
-    for i in range(n_z):
-        to_sibling(i * 4 + (1 - y) * 2 + core, 1)
+    for i in reversed(target):
+        source = i * 4 + (1 - y) * 2 + core
+        landed(gathered.at[units(source), :], across_recv.at[i])
+        to_sibling(source, 1)
     finish(n_c - 1)
-    landed(gathered.at[pl.ds(0, in_plane), :], plane_recv.at[4])
+    landed(gathered.at[pl.ds(0, in_plane), :], plane_recv.at[3])
     for i in range(n_z):
         add_gathered(i, 1 - y)
     for j in range(pieces):
@@ -505,7 +515,7 @@
             pltpu.VMEM((half, wide), bf16),
             dma((3,)), dma((11,)), dma((n_z,)), dma((n_z,)), dma((n_c,)), dma((pieces,)),
             dma((n_c + n_z - 1,)), dma((n_z + 1, n_c)),
-            dma((2, n_z - 1)), dma((2, n_z - 1)), dma((5,)),
+            dma((2, n_z - 1)), dma((2, n_z - 1)), dma((4,)), dma((n_z,)),
             pltpu.SemaphoreType.REGULAR, pltpu.SemaphoreType.REGULAR,
         ],
         compiler_params=pltpu.CompilerParams(

time: 48.8 us -> 48.4 us (level)
  no operation moved by 1% of the time
where the time goes in v4:
time: 48.4 us; the launch traced here: 48.2 us
  Pallas kernels  47.5 us (98%)
  between operations  0.64 us (1%)
    pallas_call x1, Pallas kernels, fused(): pl.pallas_call(functools.partial(kernel, n_z, pieces, n_c), out_shape=(pl...  46.3 us
    pallas_call x1, Pallas kernels, fused(): pl.pallas_call(place, out_shape=(jax.ShapeDtypeStruct((half, depth), bf16...  1.25 us

profile of v4, /device:TPU:0, one launch (start us, length us, event | category | flops | bytes accessed | tf_op | source)
XLA Modules:
  0.0 48.2 jit_solution(13813999251064009473)
XLA Ops:
  0.6 46.3 %shard_map.102 = (bf16[128,4096]{1,0:T(8,128)(2,1)S(1)}, f32[256,768]{1,0:T(8,128)S(1)}) custom-call(bf16[128,4096]{1,0:T(8,128)(2,1)} %hidden.1, bf16[256,512]{1,0:T(8,128)(2,1)} %query_grad.1, bf16[256,128]{1,0:T(8,128)(2,1)} %key_grad.1, bf16[256,128]{1,0:T(8,128)(2,1)} %value_grad.1, bf16[4096,512]{1,0:T(8,128)(2,1)} %w_query.1, ...), custom_call_target="tpu_custom_call" | custom-call | tf_op jit(solution)/shard_map/pallas_call | solution.py:497
  46.9 1.3 %shard_map.103 = (bf16[128,4096]{1,0:T(8,128)(2,1)}, f32[256,512]{1,0:T(8,128)}, f32[256,128]{1,0:T(8,128)}, f32[256,128]{1,0:T(8,128)}) custom-call(bf16[128,4096]{1,0:T(8,128)(2,1)S(1)} %get-tuple-element.6.result, f32[256,768]{1,0:T(8,128)S(1)} %get-tuple-element.7.final), custom_call_target="tpu_custom_call" | custom-call | tf_op jit(solution)/shard_map/pallas_call | solution.py:525

commit v5 on v4

--- a/solution.py
+++ b/solution.py
@@ -64,7 +64,7 @@
     tokens, grads, weights, head_out, head_in, core_out, core_in,
     total, z_out, z_in, own_head, gathered, own_grads,
     load_sem, send_sem, x_recv, ytok_recv, ygrad_recv, head_recv, core_recv, z_recv,
-    unit_send, unit_recv, plane_recv, across_recv, seen_sem, go_sem,
+    unit_recv, plane_recv, across_recv, seen_sem, go_sem,
 ):
     dp = lax.axis_index("dp")
     tp = lax.axis_index("tp")
@@ -153,14 +153,14 @@
     fwd_copies = [
         remote(
             tokens.at[k, mine_far, :], tokens.at[k, mine_far, :],
-            send_sem.at[1], x_recv.at[k], x_peer,
+            send_sem.at[0], x_recv.at[k], x_peer,
         )
         for k in range(n_z)
     ]
     ytok_copies = [
         remote(
             hidden.at[:, columns_of(k, 1 - y)], tokens.at[k, mine_far, :],
-            send_sem.at[2], ytok_recv.at[k], y_peer,
+            send_sem.at[0], ytok_recv.at[k], y_peer,
         )
         for k in range(n_z)
     ]
@@ -168,7 +168,7 @@
     def ygrad(source, first, n):
         span = pl.ds(first, source.shape[1])
         return remote(
-            source, grads.at[far, span], send_sem.at[3], ygrad_recv.at[n], y_peer
+            source, grads.at[far, span], send_sem.at[1], ygrad_recv.at[n], y_peer
         )
 
     ygrad_copies = [
@@ -177,7 +177,8 @@
     ] + [[ygrad(key_grad, q_w, n_c - 1), ygrad(value_grad, q_w + k_w, n_c - 1)]]
     head_copies = [
         remote(
-            head_out.at[j], head_in.at[j], send_sem.at[4], head_recv.at[j], x_peer
+            head_out.at[j], head_in.at[j], send_sem.at[0],
+            head_recv.at[0 if j < pieces - 1 else 1], x_peer,
         )
         for j in range(pieces)
     ]
@@ -185,7 +186,7 @@
         [
             remote(
                 core_out.at[k, n], core_in.at[k, n],
-                send_sem.at[5], core_recv.at[n if k == 0 else n_c + k - 1], core_peer,
+                send_sem.at[2], core_recv.at[n if k == 0 else n_c + k - 1], core_peer,
             )
             for n in range(n_c)
         ]
@@ -205,7 +206,7 @@
         [
             remote(
                 z_out.at[k, n], z_in.at[z_slot[k], n],
-                send_sem.at[6], z_recv.at[z_slot[k], n],
+                send_sem.at[3], z_recv.at[z_slot[k], n],
                 (dp + 4 - 8 * down[k], tp),
             )
             for n in range(n_c)
@@ -220,32 +221,32 @@
         remote(
             source.at[units(dp), :],
             gathered.at[units(dp), pl.ds(first, source.shape[1])],
-            send_sem.at[7], plane_recv.at[0], x_peer,
+            send_sem.at[1], plane_recv.at[0], x_peer,
         )
         for source, first in ((w_query, 0), (w_key, q_w), (w_value, q_w + k_w))
     ]
     lend_grads = remote(
-        grads.at[theirs, :], own_grads, send_sem.at[8], plane_recv.at[1], x_peer
+        grads.at[theirs, :], own_grads, send_sem.at[1], plane_recv.at[1], x_peer
     )
 
     def unit_copy(direction, s):
         rows_of = units(dp - 4 * s if direction == 0 else dp + 4 * s)
         return remote(
             gathered.at[rows_of, :], gathered.at[rows_of, :],
-            unit_send.at[direction, s], unit_recv.at[direction, s],
+            send_sem.at[4], unit_recv.at[z - s if direction == 0 else z + s],
             high_peer if direction == 0 else low_peer,
         )
 
     def to_sibling(source, across):
         remote(
             gathered.at[units(source), :], gathered.at[units(source), :],
-            send_sem.at[10], plane_recv.at[2 + across], core_peer,
+            send_sem.at[1], plane_recv.at[2 + across], core_peer,
         ).start()
 
     def to_plane(source):
         remote(
             gathered.at[units(source), :], gathered.at[units(source), :],
-            send_sem.at[9], across_recv.at[source // 4], y_peer,
+            send_sem.at[1], across_recv.at[source // 4], y_peer,
         ).start()
         to_sibling(source, 0)
 
@@ -255,7 +256,7 @@
     def loaded(index, whole):
         pltpu.make_async_copy(whole, whole, load_sem.at[index]).wait()
 
-    for copy in own_copies[:1] + fetches:
+    for copy in fetches + own_copies[:1]:
         copy.start()
 
     def start_later_y():
@@ -335,7 +336,10 @@
                 final[:, span] += z_in[slot, n].astype(f32)
 
     def add_heads(j):
-        head_copies[j].wait_recv()
+        if j == 0:
+            landed(head_in.at[pl.ds(0, pieces - 1)], head_recv.at[0])
+        elif j == pieces - 1:
+            landed(head_in.at[j], head_recv.at[1])
         columns = pl.ds(own_first + j * width, width)
         own = own_head[:, columns]
         result[:, columns] = (own + head_in[j].astype(f32)).astype(result.dtype)
@@ -356,7 +360,7 @@
                 spread(direction, s, onward, dp + step * s)
 
     def spread(direction, s, onward, source):
-        landed(gathered.at[units(source), :], unit_recv.at[direction, s - 1])
+        landed(gathered.at[units(source), :], unit_recv.at[z - s if direction == 0 else z + s])
         if s < n_z - 1:
             pl.when(onward)(unit_copy(direction, s).start)
         to_plane(source)
@@ -394,12 +398,11 @@
     pl.when(scout)(start_later_y)
     prepare(1)
     forward_tokens(0)
-    prepare(1)
     landed(gathered.at[units(dp), :], plane_recv.at[0])
     pl.when(jnp.logical_not(at_high))(unit_copy(0, 0).start)
     pl.when(jnp.logical_not(at_low))(unit_copy(1, 0).start)
     to_plane(dp)
-    prepare(pieces)
+    prepare(2)
     arrive(0)
     partial(0, 0)
     forward_tokens(1)
@@ -444,23 +447,14 @@
         add_gathered(i, 1 - y)
     for j in range(pieces):
         add_heads(j)
-    for s in range(n_z - 1):
-        for direction, sent_on in (
-            (0, jnp.logical_and(z >= s, jnp.logical_not(at_high))),
-            (1, jnp.logical_and(z <= n_z - 1 - s, jnp.logical_not(at_low))),
-        ):
-            @pl.when(sent_on)
-            def _():
-                landed(gathered.at[units(dp), :], unit_send.at[direction, s])
-
-    sources = (
-        tokens.at[:, mine, :], tokens.at[:, mine, :], tokens.at[:, mine, :],
-        grads.at[near, :], head_out, core_out, z_out,
-        gathered.at[units(dp), :], own_grads, gathered.at[pl.ds(0, n_z * unit), :],
-        gathered.at[pl.ds(0, 2 * n_z * unit), :],
-    )
+    units_sent = gathered.at[pl.ds(0, (3 * n_z + 4) * unit), :]
+    sources = (tokens, units_sent, core_out, z_out)
     for i, source in enumerate(sources):
         landed(source, send_sem.at[i])
+    for count, here in ((1, at_end), (n_z + 1, jnp.logical_not(at_end))):
+        pl.when(here)(
+            lambda: landed(gathered.at[pl.ds(0, count * unit), :], send_sem.at[4])
+        )
 
 
 def place(result, final, out_hidden, out_query, out_key, out_value, sem):
@@ -485,7 +479,7 @@
     q_w, k_w = w_query.shape[1], w_key.shape[1]
     wide = q_w + 2 * k_w
     rows = depth // n_dp
-    if q_w % (2 * k_w) or rows % 256 or k_w % 128 or half * 2 != group:
+    if q_w % (2 * k_w) or rows != group or rows % 256 or k_w % 128:
         return local(hidden, query_grad, key_grad, value_grad, w_query, w_key, w_value)
     n_z = n_dp // 4
     n_c = wide // (2 * k_w)
@@ -513,9 +507,9 @@
             pltpu.VMEM((half, depth), f32),
             pltpu.VMEM((depth // 2, wide), bf16),
             pltpu.VMEM((half, wide), bf16),
-            dma((3,)), dma((11,)), dma((n_z,)), dma((n_z,)), dma((n_c,)), dma((pieces,)),
+            dma((3,)), dma((5,)), dma((n_z,)), dma((n_z,)), dma((n_c,)), dma((2,)),
             dma((n_c + n_z - 1,)), dma((n_z + 1, n_c)),
-            dma((2, n_z - 1)), dma((2, n_z - 1)), dma((4,)), dma((n_z,)),
+            dma((n_z,)), dma((4,)), dma((n_z,)),
             pltpu.SemaphoreType.REGULAR, pltpu.SemaphoreType.REGULAR,
         ],
         compiler_params=pltpu.CompilerParams(
@@ -548,7 +542,7 @@
     )
     n_dp, n_tp = mesh.shape["dp"], mesh.shape["tp"]
     body = local
-    if n_tp == 2 and n_dp % 4 == 0 and n_dp > 8:
+    if n_tp == 2 and n_dp % 4 == 0 and n_dp > 12:
         body = functools.partial(fused, n_dp)
     return jax.shard_map(
         body,

time: 48.4 us -> 48.3 us (level)
  no operation moved by 1% of the time
where the time goes in v5:
time: 48.3 us; the launch traced here: 48 us
  Pallas kernels  47.4 us (98%)
  between operations  0.64 us (1%)
    pallas_call x1, Pallas kernels, fused(): pl.pallas_call(functools.partial(kernel, n_z, pieces, n_c), out_shape=(pl...  46.1 us
    pallas_call x1, Pallas kernels, fused(): pl.pallas_call(place, out_shape=(jax.ShapeDtypeStruct((half, depth), bf16...  1.25 us

profile of v5, /device:TPU:0, one launch (start us, length us, event | category | flops | bytes accessed | tf_op | source)
XLA Modules:
  0.0 48.0 jit_solution(6176064936900913347)
XLA Ops:
  0.6 46.1 %shard_map.102 = (bf16[128,4096]{1,0:T(8,128)(2,1)S(1)}, f32[256,768]{1,0:T(8,128)S(1)}) custom-call(bf16[128,4096]{1,0:T(8,128)(2,1)} %hidden.1, bf16[256,512]{1,0:T(8,128)(2,1)} %query_grad.1, bf16[256,128]{1,0:T(8,128)(2,1)} %key_grad.1, bf16[256,128]{1,0:T(8,128)(2,1)} %value_grad.1, bf16[4096,512]{1,0:T(8,128)(2,1)} %w_query.1, ...), custom_call_target="tpu_custom_call" | custom-call | tf_op jit(solution)/shard_map/pallas_call | solution.py:491
  46.8 1.3 %shard_map.103 = (bf16[128,4096]{1,0:T(8,128)(2,1)}, f32[256,512]{1,0:T(8,128)}, f32[256,128]{1,0:T(8,128)}, f32[256,128]{1,0:T(8,128)}) custom-call(bf16[128,4096]{1,0:T(8,128)(2,1)S(1)} %get-tuple-element.6.result, f32[256,768]{1,0:T(8,128)S(1)} %get-tuple-element.7.final), custom_call_target="tpu_custom_call" | custom-call | tf_op jit(solution)/shard_map/pallas_call | solution.py:519

commit v6 on v0

v6 whole, which is shorter than its diff:
```python
import functools

import jax
import jax.numpy as jnp
from jax import lax
from jax.experimental import pallas as pl
from jax.experimental.pallas import tpu as pltpu
from jax.sharding import PartitionSpec as P

MESH = pl.DeviceIdType.MESH


def contract_rows(left, right):
    return lax.dot_general(
        left, right, (((0,), (0,)), ((), ())), preferred_element_type=jnp.float32
    )


def contract_cols(left, right):
    return lax.dot_general(
        left, right, (((1,), (1,)), ((), ())), preferred_element_type=jnp.float32
    )


def local(hidden, query_grad, key_grad, value_grad, w_query, w_key, w_value):
    query_width = w_query.shape[1]
    head_width = w_key.shape[1]
    all_grads = jnp.concatenate((query_grad, key_grad, value_grad), axis=1)
    all_weights = jnp.concatenate((w_query, w_key, w_value), axis=1)
    total = contract_rows(lax.all_gather(hidden, "tp", axis=0, tiled=True), all_grads)
    summed = lax.psum_scatter(
        contract_cols(all_grads, all_weights).astype(jnp.bfloat16),
        "tp",
        scatter_dimension=0,
        tiled=True,
    )
    weight_grad = lax.psum_scatter(
        total.astype(jnp.bfloat16), "dp", scatter_dimension=0, tiled=True
    ).astype(jnp.float32)
    grad_query = weight_grad[:, :query_width]
    grad_key = weight_grad[:, query_width : query_width + head_width]
    grad_value = weight_grad[:, query_width + head_width :]
    return (summed, grad_query, grad_key, grad_value)


def targets(n_z, z):
    near_low = z < n_z - 1 - z
    return sorted(
        range(n_z), key=lambda t: (-abs(t - z), t if near_low else -t)
    )


def pick(values, index):
    chosen = jnp.int32(values[0])
    for i, value in enumerate(values[1:]):
        chosen = jnp.where(index == i + 1, jnp.int32(value), chosen)
    return chosen


def kernel(
    n_z, pieces, n_c,
    hidden, query_grad, key_grad, value_grad, w_query, w_key, w_value,
    result, final,
    tokens, grads, weights, head_out, head_in, core_out, core_in,
    total, z_out, z_in, own_head, gathered, own_grads,
    head_sem,
):
    half = hidden.shape[0]
    own_first = hidden.shape[1] // 2
    width = own_first // pieces
    dma = pltpu.SemaphoreType.DMA
    regular = pltpu.SemaphoreType.REGULAR

    def landed(whole, semaphore):
        pltpu.make_async_copy(whole, whole, semaphore).wait()

    def add_heads(j):
        columns = pl.ds(own_first + j * width, width)
        own = own_head[:, columns]
        result[:, columns] = (own + head_in[j].astype(jnp.float32)).astype(result.dtype)

    def scope(
        load_sem, send_sem, x_recv, ytok_recv, ygrad_recv, core_recv, z_recv,
        unit_recv, plane_recv, across_recv, seen_sem, go_sem,
    ):
        dp = lax.axis_index("dp")
        tp = lax.axis_index("tp")
        core = lax.rem(dp, 2)
        y = lax.rem(dp // 2, 2)
        z = dp // 4
        half = hidden.shape[0]
        group = query_grad.shape[0]
        q_w = query_grad.shape[1]
        k_w = key_grad.shape[1]
        rows = final.shape[0]
        pair = 2 * rows
        width = hidden.shape[1] // 2 // pieces
        own_first = hidden.shape[1] // 2
        unit = rows // 2
        chunk = 2 * k_w
        bf16, f32 = jnp.bfloat16, jnp.float32

        x_peer = (dp, 1 - tp)
        core_peer = (dp + 1 - 2 * core, tp)
        y_peer = (dp + 2 - 4 * y, tp)
        at_low, at_high = z == 0, z == n_z - 1
        at_end = jnp.logical_or(at_low, at_high)

        order = [targets(n_z, i) for i in range(n_z)]
        target = [pick([order[i][k] for i in range(n_z)], z) for k in range(n_z)]
        down = [jnp.where(target[k] < z, 1, 0) for k in range(n_z)]

        mine = pl.ds(pl.multiple_of(tp * half, half), half)
        theirs = pl.ds(pl.multiple_of((1 - tp) * half, half), half)
        mine_far = pl.ds(pl.multiple_of(group + tp * half, half), half)

        def columns_of(k, side):
            return pl.ds(pl.multiple_of((target[k] * 2 + side) * pair, pair), pair)

        def load(index, source, place):
            pltpu.make_async_copy(source, place, load_sem.at[index]).start()

        near = pl.ds(0, group)
        far = pl.ds(group, group)

        barrier = pltpu.get_barrier_semaphore()

        def greet(peer):
            pl.semaphore_signal(barrier, inc=1, device_id=peer, device_id_type=MESH)

        greet(x_peer)
        scout = core == 0
        low_peer, high_peer = (dp - 4, tp), (dp + 4, tp)
        around = 3 - jnp.where(at_end, 1, 0)

        def around_line(tell):
            tell(y_peer)
            pl.when(jnp.logical_not(at_low))(lambda: tell(low_peer))
            pl.when(jnp.logical_not(at_high))(lambda: tell(high_peer))

        pl.when(scout)(lambda: around_line(greet))
        pl.when(jnp.logical_not(scout))(lambda: greet(core_peer))
        load(0, query_grad, grads.at[near, pl.ds(0, q_w)])
        load(0, key_grad, grads.at[near, pl.ds(q_w, k_w)])
        load(0, value_grad, grads.at[near, pl.ds(q_w + k_w, k_w)])
        load(1, w_query, weights.at[:, pl.ds(0, q_w)])
        load(1, w_key, weights.at[:, pl.ds(q_w, k_w)])
        load(1, w_value, weights.at[:, pl.ds(q_w + k_w, k_w)])
        for k in range(n_z):
            load(2, hidden.at[:, columns_of(k, y)], tokens.at[k, mine, :])

        pl.semaphore_wait(barrier, 1 + jnp.where(scout, 1 + around, 0))

        def notify(semaphore, peer):
            pl.semaphore_signal(semaphore, inc=1, device_id=peer, device_id_type=MESH)

        def remote(source, place, send, recv, peer):
            return pltpu.make_async_remote_copy(
                src_ref=source, dst_ref=place, send_sem=send, recv_sem=recv,
                device_id=peer, device_id_type=MESH,
            )

        own_copies = [
            remote(
                hidden.at[:, columns_of(k, y)], tokens.at[k, mine, :],
                send_sem.at[0], x_recv.at[k], x_peer,
            )
            for k in range(n_z)
        ]
        fwd_copies = [
            remote(
                tokens.at[k, mine_far, :], tokens.at[k, mine_far, :],
                send_sem.at[0], x_recv.at[k], x_peer,
            )
            for k in range(n_z)
        ]
        ytok_copies = [
            remote(
                hidden.at[:, columns_of(k, 1 - y)], tokens.at[k, mine_far, :],
                send_sem.at[0], ytok_recv.at[k], y_peer,
            )
            for k in range(n_z)
        ]

        def ygrad(source, first, n):
            span = pl.ds(first, source.shape[1])
            return remote(
                source, grads.at[far, span], send_sem.at[1], ygrad_recv.at[n], y_peer
            )

        ygrad_copies = [
            [ygrad(query_grad.at[:, pl.ds(n * chunk, chunk)], n * chunk, n)]
            for n in range(n_c - 1)
        ] + [[ygrad(key_grad, q_w, n_c - 1), ygrad(value_grad, q_w + k_w, n_c - 1)]]
        head_copies = [
            remote(
                head_out.at[j], head_in.at[j], head_sem.at[0],
                head_sem.at[1 if j < pieces - 1 else 2], x_peer,
            )
            for j in range(pieces)
        ]
        core_copies = [
            [
                remote(
                    core_out.at[k, n], core_in.at[k, n],
                    send_sem.at[2], core_recv.at[n if k == 0 else n_c + k - 1], core_peer,
                )
                for n in range(n_c)
            ]
            for k in range(n_z)
        ]
        def place_on(step, below):
            i = below + 1 if order[below][step] > below else below - 1
            if not 0 <= i < n_z or order[below][step] == below:
                return 0
            to = order[below][step]
            if to == i:
                return n_z - 1 if below < i else n_z
            return order[i].index(to)

        z_slot = [pick([place_on(k, i) for i in range(n_z)], z) for k in range(n_z - 1)]
        z_copies = [
            [
                remote(
                    z_out.at[k, n], z_in.at[z_slot[k], n],
                    send_sem.at[3], z_recv.at[z_slot[k], n],
                    (dp + 4 - 8 * down[k], tp),
                )
                for n in range(n_c)
            ]
            for k in range(n_z - 1)
        ]

        def units(source):
            return pl.ds(pl.multiple_of(source * unit, unit), unit)

        fetches = [
            remote(
                source.at[units(dp), :],
                gathered.at[units(dp), pl.ds(first, source.shape[1])],
                send_sem.at[1], plane_recv.at[0], x_peer,
            )
            for source, first in ((w_query, 0), (w_key, q_w), (w_value, q_w + k_w))
        ]
        lend_grads = remote(
            grads.at[theirs, :], own_grads, send_sem.at[1], plane_recv.at[1], x_peer
        )

        def unit_copy(direction, s):
            rows_of = units(dp - 4 * s if direction == 0 else dp + 4 * s)
            return remote(
                gathered.at[rows_of, :], gathered.at[rows_of, :],
                send_sem.at[4], unit_recv.at[z - s if direction == 0 else z + s],
                high_peer if direction == 0 else low_peer,
            )

        def to_sibling(source, across):
            remote(
                gathered.at[units(source), :], gathered.at[units(source), :],
                send_sem.at[1], plane_recv.at[2 + across], core_peer,
            ).start()

        def to_plane(source):
            remote(
                gathered.at[units(source), :], gathered.at[units(source), :],
                send_sem.at[1], across_recv.at[source // 4], y_peer,
            ).start()
            to_sibling(source, 0)

        def loaded(index, whole):
            pltpu.make_async_copy(whole, whole, load_sem.at[index]).wait()

        for copy in fetches + own_copies[:1]:
            copy.start()

        def start_later_y():
            later = ygrad_copies[0] + ytok_copies[1:2]
            for copies in ygrad_copies[1:]:
                later = later + copies
            for copy in later + ytok_copies[2:]:
                copy.start()

        @pl.when(scout)
        def _():
            ytok_copies[0].start()
            around_line(lambda peer: notify(seen_sem, peer))
            pl.semaphore_wait(seen_sem, around)
            notify(go_sem, core_peer)

        @pl.when(jnp.logical_not(scout))
        def _():
            pl.semaphore_wait(go_sem, 1)
            ytok_copies[0].start()
            start_later_y()

        loaded(0, grads.at[near, :])
        loaded(1, weights)

        def head_piece(j):
            columns = pl.ds(own_first + j * width, width)
            head_out[j] = contract_cols(grads[theirs, :], weights[columns, :]).astype(bf16)
            own_head[:, columns] = contract_cols(grads[mine, :], weights[columns, :])
            columns = pl.ds(j * width, width)
            own_head[:, columns] = contract_cols(grads[mine, :], weights[columns, :])

        def block(k, n, which):
            start = pl.multiple_of(which * rows, rows)
            return contract_rows(
                tokens[k, :, pl.ds(start, rows)], grads[:, pl.ds(n * chunk, chunk)]
            )

        def arrive(k):
            if k == 0:
                loaded(2, tokens.at[:, mine, :])
            landed(tokens.at[k, pl.ds(0, group), :], x_recv.at[k])

        def partial(k, n):
            if k == 0:
                landed(grads.at[far, pl.ds(n * chunk, chunk)], ygrad_recv.at[n])
            core_out[k, n] = block(k, n, 1 - core).astype(bf16)
            core_copies[k][n].start()
            total[k, n] = block(k, n, core)

        def sibling_part(k, n):
            if k == 0:
                landed(core_in.at[k, n], core_recv.at[n])
            elif n == 0:
                landed(core_in.at[k], core_recv.at[n_c + k - 1])
            return core_in[k, n].astype(f32)

        def pass_on(k, n, at_line_end):
            def run():
                summed = total[k, n] + sibling_part(k, n)
                if not at_line_end:
                    landed(z_in.at[k, n], z_recv.at[k, n])
                    summed = summed + z_in[k, n].astype(f32)
                z_out[k, n] = summed.astype(bf16)
                z_copies[k][n].start()

            pl.when(at_end if at_line_end else jnp.logical_not(at_end))(run)

        def finish(n):
            span = pl.ds(n * chunk, chunk)
            final[:, span] = total[last, n] + sibling_part(last, n)

            for slot, edge in ((n_z - 1, at_low), (n_z, at_high)):
                @pl.when(jnp.logical_not(edge))
                def _():
                    landed(z_in.at[slot, n], z_recv.at[slot, n])
                    final[:, span] += z_in[slot, n].astype(f32)

        def add_gathered(i, side):
            start = pl.multiple_of((i * 4 + side * 2) * unit, 2 * unit)
            columns = pl.ds(start, 2 * unit)
            other = contract_cols(own_grads[...], gathered[columns, :])
            result[:, columns] = (own_head[:, columns] + other).astype(result.dtype)

        def relay(s):
            for direction, exists, onward, step in (
                (0, z >= s, jnp.logical_not(at_high), -4),
                (1, z <= n_z - 1 - s, jnp.logical_not(at_low), 4),
            ):
                @pl.when(exists)
                def _():
                    spread(direction, s, onward, dp + step * s)

        def spread(direction, s, onward, source):
            landed(gathered.at[units(source), :], unit_recv.at[z - s if direction == 0 else z + s])
            if s < n_z - 1:
                pl.when(onward)(unit_copy(direction, s).start)
            to_plane(source)

        chunks = range(n_c)
        ready = sent = 0

        def prepare(count):
            nonlocal ready
            for j in range(ready, min(ready + count, pieces)):
                head_piece(j)
            ready = min(ready + count, pieces)

        def send_heads(count):
            nonlocal sent
            for j in range(sent, min(sent + count, ready)):
                head_copies[j].start()
            sent = min(sent + count, ready)

        last = n_z - 1
        in_plane = n_z * unit

        def forward_tokens(k):
            ytok_copies[k].wait_recv()
            fwd_copies[k].start()
            for copy in own_copies[1:3] if k == 0 else own_copies[k + 1 : k + 2]:
                if k != 1:
                    copy.start()
            if k == 1:
                lend_grads.start()
            if k == last:
                send_heads(pieces)

        prepare(1)
        pl.when(scout)(start_later_y)
        prepare(1)
        forward_tokens(0)
        landed(gathered.at[units(dp), :], plane_recv.at[0])
        pl.when(jnp.logical_not(at_high))(unit_copy(0, 0).start)
        pl.when(jnp.logical_not(at_low))(unit_copy(1, 0).start)
        to_plane(dp)
        prepare(2)
        arrive(0)
        partial(0, 0)
        forward_tokens(1)
        pass_on(0, 0, True)
        for n in chunks[1:]:
            if n == n_c - 1:
                relay(1)
            partial(0, n)
            pass_on(0, n, True)
        pass_on(0, 0, False)
        for k in range(1, last):
            forward_tokens(k + 1)
            arrive(k)
            for n in chunks:
                partial(k, n)
            for n in chunks:
                pass_on(k, n, True)
            for n in chunks[1:]:
                pass_on(k - 1, n, False)
            pass_on(k, 0, False)
            if k + 1 < last:
                relay(k + 1)
        for n in chunks[1:]:
            pass_on(last - 1, n, False)
        relay(last)
        arrive(last)
        for n in chunks:
            partial(last, n)
        landed(own_grads, plane_recv.at[1])
        landed(gathered.at[pl.ds(0, in_plane), :], plane_recv.at[2])
        for i in range(n_z):
            add_gathered(i, y)
        for n in chunks[:-1]:
            finish(n)
        for i in reversed(target):
            source = i * 4 + (1 - y) * 2 + core
            landed(gathered.at[units(source), :], across_recv.at[i])
            to_sibling(source, 1)
        finish(n_c - 1)
        landed(gathered.at[pl.ds(0, in_plane), :], plane_recv.at[3])
        for i in range(n_z):
            add_gathered(i, 1 - y)
        units_sent = gathered.at[pl.ds(0, (3 * n_z + 4) * unit), :]
        sources = (tokens.at[:, pl.ds(0, 3 * half), :], units_sent, core_out, z_out)
        for i, source in enumerate(sources):
            landed(source, send_sem.at[i])
        for count, here in ((1, at_end), (n_z + 1, jnp.logical_not(at_end))):
            pl.when(here)(
                lambda: landed(gathered.at[pl.ds(0, count * unit), :], send_sem.at[4])
            )

    pl.run_scoped(
        scope,
        dma((3,)), dma((5,)), dma((n_z,)), dma((n_z,)), dma((n_c,)),
        dma((n_c + n_z - 1,)), dma((n_z + 1, n_c)),
        dma((n_z,)), dma((4,)), dma((n_z,)), regular, regular,
    )
    landed(head_in.at[pl.ds(0, pieces - 1)], head_sem.at[1])
    for j in range(pieces - 1):
        add_heads(j)
    landed(head_in.at[pieces - 1], head_sem.at[2])
    add_heads(pieces - 1)
    landed(head_out, head_sem.at[0])


def place(result, final, out_hidden, out_query, out_key, out_value, sem):
    q_w, k_w = out_query.shape[1], out_key.shape[1]
    copies = [
        pltpu.make_async_copy(result, out_hidden, sem.at[0]),
        pltpu.make_async_copy(final.at[:, pl.ds(0, q_w)], out_query, sem.at[1]),
        pltpu.make_async_copy(final.at[:, pl.ds(q_w, k_w)], out_key, sem.at[2]),
        pltpu.make_async_copy(
            final.at[:, pl.ds(q_w + k_w, k_w)], out_value, sem.at[3]
        ),
    ]
    for copy in copies:
        copy.start()
    for copy in copies:
        copy.wait()


def fused(n_dp, hidden, query_grad, key_grad, value_grad, w_query, w_key, w_value):
    half, depth = hidden.shape
    group = query_grad.shape[0]
    q_w, k_w = w_query.shape[1], w_key.shape[1]
    wide = q_w + 2 * k_w
    rows = depth // n_dp
    if q_w % (2 * k_w) or rows != group or rows % 256 or k_w % 128:
        return local(hidden, query_grad, key_grad, value_grad, w_query, w_key, w_value)
    n_z = n_dp // 4
    n_c = wide // (2 * k_w)
    chunk = 2 * k_w
    pieces = n_z
    width = depth // 2 // pieces
    bf16, f32 = jnp.bfloat16, jnp.float32
    dma = pltpu.SemaphoreType.DMA
    held = pl.pallas_call(
        functools.partial(kernel, n_z, pieces, n_c),
        out_shape=(pltpu.VMEM((half, depth), bf16), pltpu.VMEM((rows, wide), f32)),
        in_specs=[pl.BlockSpec(memory_space=pl.ANY)] * 7,
        out_specs=(pl.BlockSpec(memory_space=pltpu.VMEM),) * 2,
        scratch_shapes=[
            pltpu.VMEM((n_z, 2 * group, 2 * rows), bf16),
            pltpu.VMEM((2 * group, wide), bf16),
            pltpu.VMEM((depth, wide), bf16),
            pltpu.VMEM((pieces, half, width), bf16),
            pltpu.VMEM((pieces, half, width), bf16),
            pltpu.VMEM((n_z, n_c, rows, chunk), bf16),
            pltpu.VMEM((n_z, n_c, rows, chunk), bf16),
            pltpu.VMEM((n_z, n_c, rows, chunk), f32),
            pltpu.VMEM((n_z - 1, n_c, rows, chunk), bf16),
            pltpu.VMEM((n_z + 1, n_c, rows, chunk), bf16),
            pltpu.VMEM((half, depth), f32),
            pltpu.VMEM((depth // 2, wide), bf16),
            pltpu.VMEM((half, wide), bf16),
            dma((3,)),
        ],
        compiler_params=pltpu.CompilerParams(
            collective_id=0, has_side_effects=True, vmem_limit_bytes=56 * 1024 * 1024
        ),
    )(hidden, query_grad, key_grad, value_grad, w_query, w_key, w_value)
    return pl.pallas_call(
        place,
        out_shape=(
            jax.ShapeDtypeStruct((half, depth), bf16),
            jax.ShapeDtypeStruct((rows, q_w), f32),
            jax.ShapeDtypeStruct((rows, k_w), f32),
            jax.ShapeDtypeStruct((rows, k_w), f32),
        ),
        in_specs=[pl.BlockSpec(memory_space=pltpu.VMEM)] * 2,
        out_specs=(pl.BlockSpec(memory_space=pl.ANY),) * 4,
        scratch_shapes=[dma((4,))],
    )(*[pltpu.with_memory_space_constraint(a, pltpu.VMEM) for a in held])


def solution(mesh):
    placed = (
        P(("dp", "tp"), None),
        P("dp", "tp"),
        P("dp", "tp"),
        P("dp", "tp"),
        P(None, "tp"),
        P(None, "tp"),
        P(None, "tp"),
    )
    n_dp, n_tp = mesh.shape["dp"], mesh.shape["tp"]
    body = local
    if n_tp == 2 and n_dp % 4 == 0 and n_dp > 12:
        body = functools.partial(fused, n_dp)
    return jax.shard_map(
        body,
        mesh=mesh,
        in_specs=placed,
        out_specs=(P(("dp", "tp"), None), P("dp", "tp"), P("dp", "tp"), P("dp", "tp")),
        check_vma=False,
    )
```

time: 56.7 us -> 47.8 us (0.84)
  Pallas kernels: 55.9 us -> 46.9 us
    pallas_call x1, Pallas kernels: 54.7 us -> 45.6 us  [fused(): pl.pallas_call(functools.partial(kernel, n_z, pieces, n_c), out_shape=(pl...]
where the time goes in v6:
time: 47.8 us; the launch traced here: 47.5 us
  Pallas kernels  46.9 us (98%)
  between operations  0.64 us (1%)
    pallas_call x1, Pallas kernels, fused(): pl.pallas_call(functools.partial(kernel, n_z, pieces, n_c), out_shape=(pl...  45.6 us
    pallas_call x1, Pallas kernels, fused(): pl.pallas_call(place, out_shape=(jax.ShapeDtypeStruct((half, depth), bf16...  1.25 us

profile of v6, /device:TPU:0, one launch (start us, length us, event | category | flops | bytes accessed | tf_op | source)
XLA Modules:
  0.0 47.5 jit_solution(11211092178814602202)
XLA Ops:
  0.6 45.6 %shard_map.102 = (bf16[128,4096]{1,0:T(8,128)(2,1)S(1)}, f32[256,768]{1,0:T(8,128)S(1)}) custom-call(bf16[128,4096]{1,0:T(8,128)(2,1)} %hidden.1, bf16[256,512]{1,0:T(8,128)(2,1)} %query_grad.1, bf16[256,128]{1,0:T(8,128)(2,1)} %key_grad.1, bf16[256,128]{1,0:T(8,128)(2,1)} %value_grad.1, bf16[4096,512]{1,0:T(8,128)(2,1)} %w_query.1, ...), custom_call_target="tpu_custom_call" | custom-call | tf_op jit(solution)/shard_map/pallas_call | solution.py:507
  46.3 1.3 %shard_map.103 = (bf16[128,4096]{1,0:T(8,128)(2,1)}, f32[256,512]{1,0:T(8,128)}, f32[256,128]{1,0:T(8,128)}, f32[256,128]{1,0:T(8,128)}) custom-call(bf16[128,4096]{1,0:T(8,128)(2,1)S(1)} %get-tuple-element.6.result, f32[256,768]{1,0:T(8,128)S(1)} %get-tuple-element.7.final), custom_call_target="tpu_custom_call" | custom-call | tf_op jit(solution)/shard_map/pallas_call | solution.py:532

commit v7 on v6

--- a/solution.py
+++ b/solution.py
@@ -140,15 +140,17 @@
 
         pl.when(scout)(lambda: around_line(greet))
         pl.when(jnp.logical_not(scout))(lambda: greet(core_peer))
-        load(0, query_grad, grads.at[near, pl.ds(0, q_w)])
-        load(0, key_grad, grads.at[near, pl.ds(q_w, k_w)])
-        load(0, value_grad, grads.at[near, pl.ds(q_w + k_w, k_w)])
-        load(1, w_query, weights.at[:, pl.ds(0, q_w)])
-        load(1, w_key, weights.at[:, pl.ds(q_w, k_w)])
-        load(1, w_value, weights.at[:, pl.ds(q_w + k_w, k_w)])
-        for k in range(n_z):
-            load(2, hidden.at[:, columns_of(k, y)], tokens.at[k, mine, :])
-
+        def start_loads():
+            load(0, query_grad, grads.at[near, pl.ds(0, q_w)])
+            load(0, key_grad, grads.at[near, pl.ds(q_w, k_w)])
+            load(0, value_grad, grads.at[near, pl.ds(q_w + k_w, k_w)])
+            load(1, w_query, weights.at[:, pl.ds(0, q_w)])
+            load(1, w_key, weights.at[:, pl.ds(q_w, k_w)])
+            load(1, w_value, weights.at[:, pl.ds(q_w + k_w, k_w)])
+            for k in range(n_z):
+                load(2, hidden.at[:, columns_of(k, y)], tokens.at[k, mine, :])
+
+        pl.when(scout)(start_loads)
         pl.semaphore_wait(barrier, 1 + jnp.where(scout, 1 + around, 0))
 
         def notify(semaphore, peer):
@@ -270,8 +272,9 @@
         def loaded(index, whole):
             pltpu.make_async_copy(whole, whole, load_sem.at[index]).wait()
 
-        for copy in fetches + own_copies[:1]:
+        for copy in own_copies[:1] + fetches:
             copy.start()
+        pl.when(jnp.logical_not(scout))(start_loads)
 
         def start_later_y():
             later = ygrad_copies[0] + ytok_copies[1:2]
@@ -473,20 +476,26 @@
     landed(head_out, head_sem.at[0])
 
 
-def place(result, final, out_hidden, out_query, out_key, out_value, sem):
+def place(result, final, out_hidden, out_query, out_key, out_value):
     q_w, k_w = out_query.shape[1], out_key.shape[1]
-    copies = [
-        pltpu.make_async_copy(result, out_hidden, sem.at[0]),
-        pltpu.make_async_copy(final.at[:, pl.ds(0, q_w)], out_query, sem.at[1]),
-        pltpu.make_async_copy(final.at[:, pl.ds(q_w, k_w)], out_key, sem.at[2]),
-        pltpu.make_async_copy(
-            final.at[:, pl.ds(q_w + k_w, k_w)], out_value, sem.at[3]
-        ),
-    ]
-    for copy in copies:
-        copy.start()
-    for copy in copies:
-        copy.wait()
+
+    def scope(sem):
+        pairs = (
+            (result, out_hidden),
+            (final.at[:, pl.ds(0, q_w)], out_query),
+            (final.at[:, pl.ds(q_w, k_w)], out_key),
+            (final.at[:, pl.ds(q_w + k_w, k_w)], out_value),
+        )
+        copies = [
+            pltpu.make_async_copy(source, out, sem.at[i])
+            for i, (source, out) in enumerate(pairs)
+        ]
+        for copy in copies:
+            copy.start()
+        for copy in copies:
+            copy.wait()
+
+    pl.run_scoped(scope, pltpu.SemaphoreType.DMA((4,)))
 
 
 def fused(n_dp, hidden, query_grad, key_grad, value_grad, w_query, w_key, w_value):
@@ -539,7 +548,6 @@
         ),
         in_specs=[pl.BlockSpec(memory_space=pltpu.VMEM)] * 2,
         out_specs=(pl.BlockSpec(memory_space=pl.ANY),) * 4,
-        scratch_shapes=[dma((4,))],
     )(*[pltpu.with_memory_space_constraint(a, pltpu.VMEM) for a in held])
 
 

time: 47.8 us -> 47.8 us (level)
  no operation moved by 1% of the time
where the time goes in v7:
time: 47.8 us; the launch traced here: 47.5 us
  Pallas kernels  46.9 us (98%)
  between operations  0.64 us (1%)
    pallas_call x1, Pallas kernels, fused(): pl.pallas_call(functools.partial(kernel, n_z, pieces, n_c), out_shape=(pl...  45.6 us
    pallas_call x1, Pallas kernels, fused(): pl.pallas_call(place, out_shape=(jax.ShapeDtypeStruct((half, depth), bf16...  1.22 us

profile of v7, /device:TPU:0, one launch (start us, length us, event | category | flops | bytes accessed | tf_op | source)
XLA Modules:
  0.0 47.5 jit_solution(15447942335820073839)
XLA Ops:
  0.6 45.6 %shard_map.102 = (bf16[128,4096]{1,0:T(8,128)(2,1)S(1)}, f32[256,768]{1,0:T(8,128)S(1)}) custom-call(bf16[128,4096]{1,0:T(8,128)(2,1)} %hidden.1, bf16[256,512]{1,0:T(8,128)(2,1)} %query_grad.1, bf16[256,128]{1,0:T(8,128)(2,1)} %key_grad.1, bf16[256,128]{1,0:T(8,128)(2,1)} %value_grad.1, bf16[4096,512]{1,0:T(8,128)(2,1)} %w_query.1, ...), custom_call_target="tpu_custom_call" | custom-call | tf_op jit(solution)/shard_map/pallas_call | solution.py:516
  46.3 1.2 %shard_map.103 = (bf16[128,4096]{1,0:T(8,128)(2,1)}, f32[256,512]{1,0:T(8,128)}, f32[256,128]{1,0:T(8,128)}, f32[256,128]{1,0:T(8,128)}) custom-call(bf16[128,4096]{1,0:T(8,128)(2,1)S(1)} %get-tuple-element.6.result, f32[256,768]{1,0:T(8,128)S(1)} %get-tuple-element.7.final), custom_call_target="tpu_custom_call" | custom-call | tf_op jit(solution)/shard_map/pallas_call | solution.py:541

commit v8 on v7

--- a/solution.py
+++ b/solution.py
@@ -63,7 +63,6 @@
     result, final,
     tokens, grads, weights, head_out, head_in, core_out, core_in,
     total, z_out, z_in, own_head, gathered, own_grads,
-    head_sem,
 ):
     half = hidden.shape[0]
     own_first = hidden.shape[1] // 2
@@ -82,6 +81,7 @@
     def scope(
         load_sem, send_sem, x_recv, ytok_recv, ygrad_recv, core_recv, z_recv,
         unit_recv, plane_recv, across_recv, seen_sem, go_sem,
+        head_sem,
     ):
         dp = lax.axis_index("dp")
         tp = lax.axis_index("tp")
@@ -461,19 +461,19 @@
             pl.when(here)(
                 lambda: landed(gathered.at[pl.ds(0, count * unit), :], send_sem.at[4])
             )
+        landed(head_in.at[pl.ds(0, pieces - 1)], head_sem.at[1])
+        for j in range(pieces - 1):
+            add_heads(j)
+        landed(head_in.at[pieces - 1], head_sem.at[2])
+        add_heads(pieces - 1)
+        landed(head_out, head_sem.at[0])
 
     pl.run_scoped(
         scope,
         dma((3,)), dma((5,)), dma((n_z,)), dma((n_z,)), dma((n_c,)),
         dma((n_c + n_z - 1,)), dma((n_z + 1, n_c)),
-        dma((n_z,)), dma((4,)), dma((n_z,)), regular, regular,
-    )
-    landed(head_in.at[pl.ds(0, pieces - 1)], head_sem.at[1])
-    for j in range(pieces - 1):
-        add_heads(j)
-    landed(head_in.at[pieces - 1], head_sem.at[2])
-    add_heads(pieces - 1)
-    landed(head_out, head_sem.at[0])
+        dma((n_z,)), dma((4,)), dma((n_z,)), regular, regular, dma((3,)),
+    )
 
 
 def place(result, final, out_hidden, out_query, out_key, out_value):
@@ -532,7 +532,6 @@
             pltpu.VMEM((half, depth), f32),
             pltpu.VMEM((depth // 2, wide), bf16),
             pltpu.VMEM((half, wide), bf16),
-            dma((3,)),
         ],
         compiler_params=pltpu.CompilerParams(
             collective_id=0, has_side_effects=True, vmem_limit_bytes=56 * 1024 * 1024

time: 47.8 us -> 47.7 us (level)
  no operation moved by 1% of the time
where the time goes in v8:
time: 47.7 us; the launch traced here: 47.5 us
  Pallas kernels  46.8 us (98%)
  between operations  0.64 us (1%)
    pallas_call x1, Pallas kernels, fused(): pl.pallas_call(functools.partial(kernel, n_z, pieces, n_c), out_shape=(pl...  45.6 us
    pallas_call x1, Pallas kernels, fused(): pl.pallas_call(place, out_shape=(jax.ShapeDtypeStruct((half, depth), bf16...  1.22 us

profile of v8, /device:TPU:0, one launch (start us, length us, event | category | flops | bytes accessed | tf_op | source)
XLA Modules:
  0.0 47.5 jit_solution(17503475205646906208)
XLA Ops:
  0.6 45.6 %shard_map.102 = (bf16[128,4096]{1,0:T(8,128)(2,1)S(1)}, f32[256,768]{1,0:T(8,128)S(1)}) custom-call(bf16[128,4096]{1,0:T(8,128)(2,1)} %hidden.1, bf16[256,512]{1,0:T(8,128)(2,1)} %query_grad.1, bf16[256,128]{1,0:T(8,128)(2,1)} %key_grad.1, bf16[256,128]{1,0:T(8,128)(2,1)} %value_grad.1, bf16[4096,512]{1,0:T(8,128)(2,1)} %w_query.1, ...), custom_call_target="tpu_custom_call" | custom-call | tf_op jit(solution)/shard_map/pallas_call | solution.py:516
  46.3 1.2 %shard_map.103 = (bf16[128,4096]{1,0:T(8,128)(2,1)}, f32[256,512]{1,0:T(8,128)}, f32[256,128]{1,0:T(8,128)}, f32[256,128]{1,0:T(8,128)}) custom-call(bf16[128,4096]{1,0:T(8,128)(2,1)S(1)} %get-tuple-element.6.result, f32[256,768]{1,0:T(8,128)S(1)} %get-tuple-element.7.final), custom_call_target="tpu_custom_call" | custom-call | tf_op jit(solution)/shard_map/pallas_call | solution.py:540
